TPU v7x, 8 devices: a whole 2x2x1 slice. The times are simulated.
8 devices in a mesh: fsdp: 8 (over z, y, x, core).
Axes of the slice: x: 2, y: 2, z: 1, core: 2. Of those that a mesh axis runs over, the one named last changes fastest.
Arguments:
- hidden: bfloat16 [16384, 1280], P('fsdp')
- targets: int32 [16384], P('fsdp')
- resp_mask: int32 [16384], P('fsdp')
- resp_id: int32 [16384], P('fsdp')
- old_logp: float32 [16384], P('fsdp')
- ref_logp: float32 [16384], P('fsdp')
- rewards: float32 [128], P('fsdp')
- prompt_id: int32 [128], P('fsdp')
- norm_w: bfloat16 [1280], P('fsdp')
- embedding: bfloat16 [32000, 1280], P('fsdp')
Outputs:
- output 1: float32 [], replicated
- output 2: bfloat16 [16384, 1280], P('fsdp')
- output 3: float32 [32000, 1280], P('fsdp')
- output 4: float32 [1280], P('fsdp')
All inputs are finite; a program needn't handle non-finite values.
Results may differ from a plain program's by a relative error of at most 0.001.
Values are sent between devices in bfloat16 or wider.
A program may use at most 1 GiB of HBM per device.

v0:
```python
import jax
import jax.numpy as jnp
from jax import lax
from jax.sharding import PartitionSpec as P

GROUP_SIZE = 8
CLIP_LOW = 0.8
CLIP_HIGH = 1.28
KL_COEF = 0.04
EPSILON = 1e-6
MAX_BLOCK = 256


def token_terms(tok_logp, old_block, ref_block, adv_block):
    ratio = jnp.exp(tok_logp - old_block)
    surr_raw = ratio * adv_block
    surr_clip = jnp.clip(ratio, CLIP_LOW, CLIP_HIGH) * adv_block
    kl_gap = ref_block - tok_logp
    tok_loss = -jnp.minimum(surr_raw, surr_clip) + KL_COEF * (jnp.exp(kl_gap) - kl_gap - 1.0)
    keep = (surr_raw <= surr_clip) | ((ratio > CLIP_LOW) & (ratio < CLIP_HIGH))
    d_logp = -jnp.where(keep, surr_raw, 0.0) + KL_COEF * (1.0 - jnp.exp(kl_gap))
    return tok_loss, d_logp


def solution(mesh):
    shards = mesh.shape['fsdp']

    def local(hidden, targets, resp_mask, resp_id, old_logp, ref_logp, rewards, prompt_id, norm_w, embedding):
        tok_dev, model_dim = hidden.shape
        prompts = rewards.shape[0] * shards // GROUP_SIZE
        emb_full = lax.all_gather(embedding, 'fsdp', tiled=True)
        gain = lax.all_gather(norm_w, 'fsdp', tiled=True).astype(jnp.float32)
        rew_stats = jnp.stack([rewards, rewards * rewards, jnp.ones_like(rewards)], axis=1)
        totals = lax.psum(jax.ops.segment_sum(rew_stats, prompt_id, num_segments=prompts), 'fsdp')
        mask_f = resp_mask.astype(jnp.float32)
        count = lax.psum(jnp.sum(mask_f), 'fsdp')
        mean_r = totals[:, 0] / totals[:, 2]
        std_r = jnp.sqrt(jnp.maximum(totals[:, 1] / totals[:, 2] - mean_r * mean_r, 0.0))
        adv_resp = (rewards - mean_r[prompt_id]) / (std_r[prompt_id] + EPSILON)
        adv_tok = adv_resp[resp_id]
        hid_f32 = hidden.astype(jnp.float32)
        inv_rms = lax.rsqrt(jnp.mean(hid_f32 * hid_f32, axis=-1, keepdims=True) + EPSILON)
        normed = hid_f32 * inv_rms
        x_rows = (normed * gain).astype(jnp.bfloat16)
        vocab_ids = jnp.arange(emb_full.shape[0], dtype=jnp.int32)
        block_len = min(tok_dev, MAX_BLOCK)
        n_blocks = tok_dev // block_len

        def step(grad_emb, pack):
            x_block, tgt_block, mask_block, old_block, ref_block, adv_block = pack
            logits = lax.dot_general(x_block, emb_full, (((1,), (1,)), ((), ())), preferred_element_type=jnp.float32)
            row_max = jnp.max(logits, axis=1, keepdims=True)
            shifted = jnp.exp(logits - row_max)
            sum_exp = jnp.sum(shifted, axis=1, keepdims=True)
            is_target = vocab_ids[None, :] == tgt_block[:, None]
            tok_logp = jnp.sum(jnp.where(is_target, logits, 0.0), axis=1) - (row_max + jnp.log(sum_exp))[:, 0]
            tok_loss, d_logp = token_terms(tok_logp, old_block, ref_block, adv_block)
            tok_coef = (mask_block * d_logp / count)[:, None]
            d_logits = (tok_coef * (jnp.where(is_target, 1.0, 0.0) - shifted / sum_exp)).astype(jnp.bfloat16)
            dx_block = jnp.dot(d_logits, emb_full, preferred_element_type=jnp.float32)
            grad_emb = grad_emb + lax.dot_general(d_logits, x_block, (((0,), (0,)), ((), ())), preferred_element_type=jnp.float32)
            return grad_emb, (jnp.sum(mask_block * tok_loss), dx_block)

        pack = (x_rows.reshape(n_blocks, block_len, model_dim), targets.reshape(n_blocks, block_len), mask_f.reshape(n_blocks, block_len), old_logp.reshape(n_blocks, block_len), ref_logp.reshape(n_blocks, block_len), adv_tok.reshape(n_blocks, block_len))
        grad_full, (loss_parts, dx_blocks) = lax.scan(step, jnp.zeros(emb_full.shape, jnp.float32), pack)
        d_embedding = lax.psum_scatter(grad_full, 'fsdp', scatter_dimension=0, tiled=True)
        d_x = dx_blocks.reshape(tok_dev, model_dim)
        d_norm_w = lax.psum_scatter(jnp.sum(d_x * normed, axis=0), 'fsdp', scatter_dimension=0, tiled=True)
        d_normed = d_x * gain
        d_hidden = (inv_rms * (d_normed - normed * jnp.mean(d_normed * normed, axis=-1, keepdims=True))).astype(jnp.bfloat16)
        mean_loss = lax.psum(jnp.sum(loss_parts), 'fsdp') / count
        return mean_loss, d_hidden, d_embedding, d_norm_w

    tok_spec = P('fsdp')
    row_spec = P('fsdp', None)
    return jax.shard_map(local, mesh=mesh, in_specs=(row_spec, tok_spec, tok_spec, tok_spec, tok_spec, tok_spec, tok_spec, tok_spec, tok_spec, row_spec), out_specs=(P(), row_spec, row_spec, tok_spec), check_vma=False)
```

profile of v0, /device:TPU:0, one launch (start us, length us, event | category | flops | bytes accessed | tf_op | source)
XLA Modules:
  0.0 3139.2 jit_solution(5860121175797190969)
XLA Ops:
  12.3 25.5 all-reduce.3
  53.0 24.3 all-reduce
  91.4 283.6 %all-gather.2.cloned.1.call-done = bf16[32000,1280]{1,0:T(8,128)(2,1)} async-done(((bf16[4000,1280]{1,0:T(8,128)(2,1)}), bf16[32000,1280]{1,0:T(8,128)(2,1)}) %all-gather.2.cloned.1.call-update) | async-done | bytes 81920016 | tf_op jit(solution)/shard_map/all_gather | solution.py:31
  375.0 1711.5 %while.17 = (s32[]{:T(128)}, f32[32000,1280]{1,0:T(8,128)}, f32[8]{0:T(128)}, f32[8,256,1280]{2,1,0:T(8,128)}, f32[8,256]{1,0:T(8,128)S(1)}, /*index=5*/s32[8,25...) while((s32[]{:T(128)}, f32[32000,1280]{1,0:T(8,128)}, ...), condition=%wide.region_10.11_spmd.clone, body=%wide.region_5.10_spmd.clone.sunk | while | flops 63160328192 | bytes 625378304 | solution.py:65
  375.0 43.0 %fusion.67 = (f32[256]{0:T(256)S(1)}, f32[256,32000]{1,0:T(8,128)}) fusion(bf16[32000,1280]{1,0:T(8,128)(2,1)} %get-tuple-element.397, bf16[8,256,1280]{2,1,0:T(8,128)(2,1)} %get-tuple-element.396, s32[]{:T(128)} %get-tuple-element.376), kind=kOutput, calls=%fused_computation.74.clone.1 | convolution fusion | flops 20979712000 | bytes 115344896 | tf_op jit(solution)/shard_map/while/body/eval_jaxpr/dot_general | solution.py:51
  418.7 16.2 fusion.68
  437.6 67.8 %select_add_fusion.2 = f32[32000,1280]{1,0:T(8,128)} fusion(f32[32000,1280]{1,0:T(8,128)} %get-tuple-element.377, pred[]{:T(512)S(6)} %compare.34, bf16[8,256,1280]{2,1,0:T(8,128)(2,1)} %get-tuple-element.396, s32[]{:T(128)} %get-tuple-element.376, f32[256,32000]{1,0:T(8,128)} %get-tuple-element.352, f32[256]{0:T(256)S(1)} %get-tuple-element.354, ...), kind=kOutput, calls=%fused_computation.4.clone.3 | convolution fusion | flops 21110784000 | bytes 361107968 | tf_op jit(solution)/shard_map/while/body/eval_jaxpr/dot_general | solution.py:61
  505.5 41.0 %fusion.70 = f32[8,256,1280]{2,1,0:T(8,128)} fusion(f32[8,256,1280]{2,1,0:T(8,128)} %get-tuple-element.379, s32[]{:T(128)} %get-tuple-element.376, bf16[32000,1280]{1,0:T(8,128)(2,1)} %get-tuple-element.397, f32[256,32000]{1,0:T(8,128)} %get-tuple-element.352, f32[256]{0:T(256)S(1)} %get-tuple-element.354, f32[256]{0:T(256)S(1)} %get-tuple-element.360, ...), kind=kOutput, calls=%fused_computation.15.clone.1 | convolution fusion | flops 21028864000 | bytes 116003328 | tf_op jit(solution)/shard_map/while/body/eval_jaxpr/dot_general | solution.py:60
  547.8 43.0 %fusion.67 = (f32[256]{0:T(256)S(1)}, f32[256,32000]{1,0:T(8,128)}) fusion(bf16[32000,1280]{1,0:T(8,128)(2,1)} %get-tuple-element.397, bf16[8,256,1280]{2,1,0:T(8,128)(2,1)} %get-tuple-element.396, s32[]{:T(128)} %get-tuple-element.376), kind=kOutput, calls=%fused_computation.74.clone.1 | convolution fusion | flops 20979712000 | bytes 115344896 | tf_op jit(solution)/shard_map/while/body/eval_jaxpr/dot_general | solution.py:51
  610.4 114.8 %select_add_fusion.2 = f32[32000,1280]{1,0:T(8,128)} fusion(f32[32000,1280]{1,0:T(8,128)} %get-tuple-element.377, pred[]{:T(512)S(6)} %compare.34, bf16[8,256,1280]{2,1,0:T(8,128)(2,1)} %get-tuple-element.396, s32[]{:T(128)} %get-tuple-element.376, f32[256,32000]{1,0:T(8,128)} %get-tuple-element.352, f32[256]{0:T(256)S(1)} %get-tuple-element.354, ...), kind=kOutput, calls=%fused_computation.4.clone.3 | convolution fusion | flops 21110784000 | bytes 361107968 | tf_op jit(solution)/shard_map/while/body/eval_jaxpr/dot_general | solution.py:61
  725.3 41.1 %fusion.70 = f32[8,256,1280]{2,1,0:T(8,128)} fusion(f32[8,256,1280]{2,1,0:T(8,128)} %get-tuple-element.379, s32[]{:T(128)} %get-tuple-element.376, bf16[32000,1280]{1,0:T(8,128)(2,1)} %get-tuple-element.397, f32[256,32000]{1,0:T(8,128)} %get-tuple-element.352, f32[256]{0:T(256)S(1)} %get-tuple-element.354, f32[256]{0:T(256)S(1)} %get-tuple-element.360, ...), kind=kOutput, calls=%fused_computation.15.clone.1 | convolution fusion | flops 21028864000 | bytes 116003328 | tf_op jit(solution)/shard_map/while/body/eval_jaxpr/dot_general | solution.py:60
  767.6 43.0 %fusion.67 = (f32[256]{0:T(256)S(1)}, f32[256,32000]{1,0:T(8,128)}) fusion(bf16[32000,1280]{1,0:T(8,128)(2,1)} %get-tuple-element.397, bf16[8,256,1280]{2,1,0:T(8,128)(2,1)} %get-tuple-element.396, s32[]{:T(128)} %get-tuple-element.376), kind=kOutput, calls=%fused_computation.74.clone.1 | convolution fusion | flops 20979712000 | bytes 115344896 | tf_op jit(solution)/shard_map/while/body/eval_jaxpr/dot_general | solution.py:51
  811.3 16.2 fusion.68
  830.2 114.8 %select_add_fusion.2 = f32[32000,1280]{1,0:T(8,128)} fusion(f32[32000,1280]{1,0:T(8,128)} %get-tuple-element.377, pred[]{:T(512)S(6)} %compare.34, bf16[8,256,1280]{2,1,0:T(8,128)(2,1)} %get-tuple-element.396, s32[]{:T(128)} %get-tuple-element.376, f32[256,32000]{1,0:T(8,128)} %get-tuple-element.352, f32[256]{0:T(256)S(1)} %get-tuple-element.354, ...), kind=kOutput, calls=%fused_computation.4.clone.3 | convolution fusion | flops 21110784000 | bytes 361107968 | tf_op jit(solution)/shard_map/while/body/eval_jaxpr/dot_general | solution.py:61
  945.1 41.1 %fusion.70 = f32[8,256,1280]{2,1,0:T(8,128)} fusion(f32[8,256,1280]{2,1,0:T(8,128)} %get-tuple-element.379, s32[]{:T(128)} %get-tuple-element.376, bf16[32000,1280]{1,0:T(8,128)(2,1)} %get-tuple-element.397, f32[256,32000]{1,0:T(8,128)} %get-tuple-element.352, f32[256]{0:T(256)S(1)} %get-tuple-element.354, f32[256]{0:T(256)S(1)} %get-tuple-element.360, ...), kind=kOutput, calls=%fused_computation.15.clone.1 | convolution fusion | flops 21028864000 | bytes 116003328 | tf_op jit(solution)/shard_map/while/body/eval_jaxpr/dot_general | solution.py:60
  987.5 43.0 %fusion.67 = (f32[256]{0:T(256)S(1)}, f32[256,32000]{1,0:T(8,128)}) fusion(bf16[32000,1280]{1,0:T(8,128)(2,1)} %get-tuple-element.397, bf16[8,256,1280]{2,1,0:T(8,128)(2,1)} %get-tuple-element.396, s32[]{:T(128)} %get-tuple-element.376), kind=kOutput, calls=%fused_computation.74.clone.1 | convolution fusion | flops 20979712000 | bytes 115344896 | tf_op jit(solution)/shard_map/while/body/eval_jaxpr/dot_general | solution.py:51
  1050.1 114.8 %select_add_fusion.2 = f32[32000,1280]{1,0:T(8,128)} fusion(f32[32000,1280]{1,0:T(8,128)} %get-tuple-element.377, pred[]{:T(512)S(6)} %compare.34, bf16[8,256,1280]{2,1,0:T(8,128)(2,1)} %get-tuple-element.396, s32[]{:T(128)} %get-tuple-element.376, f32[256,32000]{1,0:T(8,128)} %get-tuple-element.352, f32[256]{0:T(256)S(1)} %get-tuple-element.354, ...), kind=kOutput, calls=%fused_computation.4.clone.3 | convolution fusion | flops 21110784000 | bytes 361107968 | tf_op jit(solution)/shard_map/while/body/eval_jaxpr/dot_general | solution.py:61
  1164.9 41.0 %fusion.70 = f32[8,256,1280]{2,1,0:T(8,128)} fusion(f32[8,256,1280]{2,1,0:T(8,128)} %get-tuple-element.379, s32[]{:T(128)} %get-tuple-element.376, bf16[32000,1280]{1,0:T(8,128)(2,1)} %get-tuple-element.397, f32[256,32000]{1,0:T(8,128)} %get-tuple-element.352, f32[256]{0:T(256)S(1)} %get-tuple-element.354, f32[256]{0:T(256)S(1)} %get-tuple-element.360, ...), kind=kOutput, calls=%fused_computation.15.clone.1 | convolution fusion | flops 21028864000 | bytes 116003328 | tf_op jit(solution)/shard_map/while/body/eval_jaxpr/dot_general | solution.py:60
  1207.3 43.0 %fusion.67 = (f32[256]{0:T(256)S(1)}, f32[256,32000]{1,0:T(8,128)}) fusion(bf16[32000,1280]{1,0:T(8,128)(2,1)} %get-tuple-element.397, bf16[8,256,1280]{2,1,0:T(8,128)(2,1)} %get-tuple-element.396, s32[]{:T(128)} %get-tuple-element.376), kind=kOutput, calls=%fused_computation.74.clone.1 | convolution fusion | flops 20979712000 | bytes 115344896 | tf_op jit(solution)/shard_map/while/body/eval_jaxpr/dot_general | solution.py:51
  1269.9 114.8 %select_add_fusion.2 = f32[32000,1280]{1,0:T(8,128)} fusion(f32[32000,1280]{1,0:T(8,128)} %get-tuple-element.377, pred[]{:T(512)S(6)} %compare.34, bf16[8,256,1280]{2,1,0:T(8,128)(2,1)} %get-tuple-element.396, s32[]{:T(128)} %get-tuple-element.376, f32[256,32000]{1,0:T(8,128)} %get-tuple-element.352, f32[256]{0:T(256)S(1)} %get-tuple-element.354, ...), kind=kOutput, calls=%fused_computation.4.clone.3 | convolution fusion | flops 21110784000 | bytes 361107968 | tf_op jit(solution)/shard_map/while/body/eval_jaxpr/dot_general | solution.py:61
  1384.7 41.1 %fusion.70 = f32[8,256,1280]{2,1,0:T(8,128)} fusion(f32[8,256,1280]{2,1,0:T(8,128)} %get-tuple-element.379, s32[]{:T(128)} %get-tuple-element.376, bf16[32000,1280]{1,0:T(8,128)(2,1)} %get-tuple-element.397, f32[256,32000]{1,0:T(8,128)} %get-tuple-element.352, f32[256]{0:T(256)S(1)} %get-tuple-element.354, f32[256]{0:T(256)S(1)} %get-tuple-element.360, ...), kind=kOutput, calls=%fused_computation.15.clone.1 | convolution fusion | flops 21028864000 | bytes 116003328 | tf_op jit(solution)/shard_map/while/body/eval_jaxpr/dot_general | solution.py:60
  1427.1 43.0 %fusion.67 = (f32[256]{0:T(256)S(1)}, f32[256,32000]{1,0:T(8,128)}) fusion(bf16[32000,1280]{1,0:T(8,128)(2,1)} %get-tuple-element.397, bf16[8,256,1280]{2,1,0:T(8,128)(2,1)} %get-tuple-element.396, s32[]{:T(128)} %get-tuple-element.376), kind=kOutput, calls=%fused_computation.74.clone.1 | convolution fusion | flops 20979712000 | bytes 115344896 | tf_op jit(solution)/shard_map/while/body/eval_jaxpr/dot_general | solution.py:51
  1489.7 114.8 %select_add_fusion.2 = f32[32000,1280]{1,0:T(8,128)} fusion(f32[32000,1280]{1,0:T(8,128)} %get-tuple-element.377, pred[]{:T(512)S(6)} %compare.34, bf16[8,256,1280]{2,1,0:T(8,128)(2,1)} %get-tuple-element.396, s32[]{:T(128)} %get-tuple-element.376, f32[256,32000]{1,0:T(8,128)} %get-tuple-element.352, f32[256]{0:T(256)S(1)} %get-tuple-element.354, ...), kind=kOutput, calls=%fused_computation.4.clone.3 | convolution fusion | flops 21110784000 | bytes 361107968 | tf_op jit(solution)/shard_map/while/body/eval_jaxpr/dot_general | solution.py:61
  1604.5 41.0 %fusion.70 = f32[8,256,1280]{2,1,0:T(8,128)} fusion(f32[8,256,1280]{2,1,0:T(8,128)} %get-tuple-element.379, s32[]{:T(128)} %get-tuple-element.376, bf16[32000,1280]{1,0:T(8,128)(2,1)} %get-tuple-element.397, f32[256,32000]{1,0:T(8,128)} %get-tuple-element.352, f32[256]{0:T(256)S(1)} %get-tuple-element.354, f32[256]{0:T(256)S(1)} %get-tuple-element.360, ...), kind=kOutput, calls=%fused_computation.15.clone.1 | convolution fusion | flops 21028864000 | bytes 116003328 | tf_op jit(solution)/shard_map/while/body/eval_jaxpr/dot_general | solution.py:60
  1646.9 43.0 %fusion.67 = (f32[256]{0:T(256)S(1)}, f32[256,32000]{1,0:T(8,128)}) fusion(bf16[32000,1280]{1,0:T(8,128)(2,1)} %get-tuple-element.397, bf16[8,256,1280]{2,1,0:T(8,128)(2,1)} %get-tuple-element.396, s32[]{:T(128)} %get-tuple-element.376), kind=kOutput, calls=%fused_computation.74.clone.1 | convolution fusion | flops 20979712000 | bytes 115344896 | tf_op jit(solution)/shard_map/while/body/eval_jaxpr/dot_general | solution.py:51
  1709.5 114.8 %select_add_fusion.2 = f32[32000,1280]{1,0:T(8,128)} fusion(f32[32000,1280]{1,0:T(8,128)} %get-tuple-element.377, pred[]{:T(512)S(6)} %compare.34, bf16[8,256,1280]{2,1,0:T(8,128)(2,1)} %get-tuple-element.396, s32[]{:T(128)} %get-tuple-element.376, f32[256,32000]{1,0:T(8,128)} %get-tuple-element.352, f32[256]{0:T(256)S(1)} %get-tuple-element.354, ...), kind=kOutput, calls=%fused_computation.4.clone.3 | convolution fusion | flops 21110784000 | bytes 361107968 | tf_op jit(solution)/shard_map/while/body/eval_jaxpr/dot_general | solution.py:61
  1824.3 41.1 %fusion.70 = f32[8,256,1280]{2,1,0:T(8,128)} fusion(f32[8,256,1280]{2,1,0:T(8,128)} %get-tuple-element.379, s32[]{:T(128)} %get-tuple-element.376, bf16[32000,1280]{1,0:T(8,128)(2,1)} %get-tuple-element.397, f32[256,32000]{1,0:T(8,128)} %get-tuple-element.352, f32[256]{0:T(256)S(1)} %get-tuple-element.354, f32[256]{0:T(256)S(1)} %get-tuple-element.360, ...), kind=kOutput, calls=%fused_computation.15.clone.1 | convolution fusion | flops 21028864000 | bytes 116003328 | tf_op jit(solution)/shard_map/while/body/eval_jaxpr/dot_general | solution.py:60
  1866.7 43.0 %fusion.67 = (f32[256]{0:T(256)S(1)}, f32[256,32000]{1,0:T(8,128)}) fusion(bf16[32000,1280]{1,0:T(8,128)(2,1)} %get-tuple-element.397, bf16[8,256,1280]{2,1,0:T(8,128)(2,1)} %get-tuple-element.396, s32[]{:T(128)} %get-tuple-element.376), kind=kOutput, calls=%fused_computation.74.clone.1 | convolution fusion | flops 20979712000 | bytes 115344896 | tf_op jit(solution)/shard_map/while/body/eval_jaxpr/dot_general | solution.py:51
  1929.3 114.8 %select_add_fusion.2 = f32[32000,1280]{1,0:T(8,128)} fusion(f32[32000,1280]{1,0:T(8,128)} %get-tuple-element.377, pred[]{:T(512)S(6)} %compare.34, bf16[8,256,1280]{2,1,0:T(8,128)(2,1)} %get-tuple-element.396, s32[]{:T(128)} %get-tuple-element.376, f32[256,32000]{1,0:T(8,128)} %get-tuple-element.352, f32[256]{0:T(256)S(1)} %get-tuple-element.354, ...), kind=kOutput, calls=%fused_computation.4.clone.3 | convolution fusion | flops 21110784000 | bytes 361107968 | tf_op jit(solution)/shard_map/while/body/eval_jaxpr/dot_general | solution.py:61
  2044.1 41.1 %fusion.70 = f32[8,256,1280]{2,1,0:T(8,128)} fusion(f32[8,256,1280]{2,1,0:T(8,128)} %get-tuple-element.379, s32[]{:T(128)} %get-tuple-element.376, bf16[32000,1280]{1,0:T(8,128)(2,1)} %get-tuple-element.397, f32[256,32000]{1,0:T(8,128)} %get-tuple-element.352, f32[256]{0:T(256)S(1)} %get-tuple-element.354, f32[256]{0:T(256)S(1)} %get-tuple-element.360, ...), kind=kOutput, calls=%fused_computation.15.clone.1 | convolution fusion | flops 21028864000 | bytes 116003328 | tf_op jit(solution)/shard_map/while/body/eval_jaxpr/dot_general | solution.py:60
  2095.9 22.4 all-reduce.2
  2129.6 1001.7 %reduce-scatter.2.cloned.1.call-done = f32[4000,1280]{1,0:T(8,128)} async-done(((f32[32000,1280]{1,0:T(8,128)}), f32[4000,1280]{1,0:T(8,128)}) %reduce-scatter.2.cloned.1.call-update) | async-done | bytes 20480016 | tf_op jit(solution)/shard_map/reduce_scatter | solution.py:66
  (191 shorter events, 188.9 us)
Async XLA Ops:
  7.2 367.9 %all-gather.2.cloned.1.call-start = ((), (), s32[]{:S(2)}) async-start(), calls=%async_computation.1 | async-start | bytes 92160000 | tf_op jit(solution)/shard_map/all_gather | solution.py:31
  7.9 3123.4 %reduce-scatter.2.cloned.1.call-start = ((), (), s32[]{:S(2)}) async-start(), calls=%async_computation.2 | async-start | bytes 184320000 | tf_op jit(solution)/shard_map/reduce_scatter | solution.py:66
  77.3 297.8 %copy-start = (f32[1280]{0:T(1024)}, f32[1280]{0:T(1024)S(1)}, u32[]{:S(2)}) copy-start(f32[1280]{0:T(1024)S(1)} %convert_element_type.23) | copy-start | bytes 15364
  375.0 59.8 %copy-start.6 = (f32[8,256]{1,0:T(8,128)}, f32[8,256]{1,0:T(8,128)S(1)}, u32[]{:S(2)}) copy-start(f32[8,256]{1,0:T(8,128)S(1)} %get-tuple-element.394) | copy-start | bytes 24580 | tf_op jit(solution)/shard_map/while
  375.0 60.5 %copy-start.4 = (f32[8,256]{1,0:T(8,128)}, f32[8,256]{1,0:T(8,128)S(1)}, u32[]{:S(2)}) copy-start(f32[8,256]{1,0:T(8,128)S(1)} %get-tuple-element.399) | copy-start | bytes 24580 | tf_op jit(solution)/shard_map/while
  547.8 59.8 %copy-start.6 = (f32[8,256]{1,0:T(8,128)}, f32[8,256]{1,0:T(8,128)S(1)}, u32[]{:S(2)}) copy-start(f32[8,256]{1,0:T(8,128)S(1)} %get-tuple-element.394) | copy-start | bytes 24580 | tf_op jit(solution)/shard_map/while
  547.8 60.6 %copy-start.4 = (f32[8,256]{1,0:T(8,128)}, f32[8,256]{1,0:T(8,128)S(1)}, u32[]{:S(2)}) copy-start(f32[8,256]{1,0:T(8,128)S(1)} %get-tuple-element.399) | copy-start | bytes 24580 | tf_op jit(solution)/shard_map/while
  725.2 42.4 %copy-start.5 = (f32[8,256]{1,0:T(8,128)S(1)}, f32[8,256]{1,0:T(8,128)}, u32[]{:S(2)}) copy-start(f32[8,256]{1,0:T(8,128)} %copy-done.4) | copy-start | bytes 24580 | tf_op jit(solution)/shard_map/while
  725.2 42.4 %copy-start.7 = (f32[8,256]{1,0:T(8,128)S(1)}, f32[8,256]{1,0:T(8,128)}, u32[]{:S(2)}) copy-start(f32[8,256]{1,0:T(8,128)} %copy-done.6) | copy-start | bytes 24580 | tf_op jit(solution)/shard_map/while
  767.6 59.8 %copy-start.6 = (f32[8,256]{1,0:T(8,128)}, f32[8,256]{1,0:T(8,128)S(1)}, u32[]{:S(2)}) copy-start(f32[8,256]{1,0:T(8,128)S(1)} %get-tuple-element.394) | copy-start | bytes 24580 | tf_op jit(solution)/shard_map/while
  767.6 60.6 %copy-start.4 = (f32[8,256]{1,0:T(8,128)}, f32[8,256]{1,0:T(8,128)S(1)}, u32[]{:S(2)}) copy-start(f32[8,256]{1,0:T(8,128)S(1)} %get-tuple-element.399) | copy-start | bytes 24580 | tf_op jit(solution)/shard_map/while
  945.1 42.4 %copy-start.5 = (f32[8,256]{1,0:T(8,128)S(1)}, f32[8,256]{1,0:T(8,128)}, u32[]{:S(2)}) copy-start(f32[8,256]{1,0:T(8,128)} %copy-done.4) | copy-start | bytes 24580 | tf_op jit(solution)/shard_map/while
  945.1 42.4 %copy-start.7 = (f32[8,256]{1,0:T(8,128)S(1)}, f32[8,256]{1,0:T(8,128)}, u32[]{:S(2)}) copy-start(f32[8,256]{1,0:T(8,128)} %copy-done.6) | copy-start | bytes 24580 | tf_op jit(solution)/shard_map/while
  987.5 59.8 %copy-start.6 = (f32[8,256]{1,0:T(8,128)}, f32[8,256]{1,0:T(8,128)S(1)}, u32[]{:S(2)}) copy-start(f32[8,256]{1,0:T(8,128)S(1)} %get-tuple-element.394) | copy-start | bytes 24580 | tf_op jit(solution)/shard_map/while
  987.5 60.6 %copy-start.4 = (f32[8,256]{1,0:T(8,128)}, f32[8,256]{1,0:T(8,128)S(1)}, u32[]{:S(2)}) copy-start(f32[8,256]{1,0:T(8,128)S(1)} %get-tuple-element.399) | copy-start | bytes 24580 | tf_op jit(solution)/shard_map/while
  1164.9 42.4 %copy-start.5 = (f32[8,256]{1,0:T(8,128)S(1)}, f32[8,256]{1,0:T(8,128)}, u32[]{:S(2)}) copy-start(f32[8,256]{1,0:T(8,128)} %copy-done.4) | copy-start | bytes 24580 | tf_op jit(solution)/shard_map/while
  1164.9 42.4 %copy-start.7 = (f32[8,256]{1,0:T(8,128)S(1)}, f32[8,256]{1,0:T(8,128)}, u32[]{:S(2)}) copy-start(f32[8,256]{1,0:T(8,128)} %copy-done.6) | copy-start | bytes 24580 | tf_op jit(solution)/shard_map/while
  1207.3 59.9 %copy-start.6 = (f32[8,256]{1,0:T(8,128)}, f32[8,256]{1,0:T(8,128)S(1)}, u32[]{:S(2)}) copy-start(f32[8,256]{1,0:T(8,128)S(1)} %get-tuple-element.394) | copy-start | bytes 24580 | tf_op jit(solution)/shard_map/while
  1207.3 60.6 %copy-start.4 = (f32[8,256]{1,0:T(8,128)}, f32[8,256]{1,0:T(8,128)S(1)}, u32[]{:S(2)}) copy-start(f32[8,256]{1,0:T(8,128)S(1)} %get-tuple-element.399) | copy-start | bytes 24580 | tf_op jit(solution)/shard_map/while
  1384.7 42.4 %copy-start.5 = (f32[8,256]{1,0:T(8,128)S(1)}, f32[8,256]{1,0:T(8,128)}, u32[]{:S(2)}) copy-start(f32[8,256]{1,0:T(8,128)} %copy-done.4) | copy-start | bytes 24580 | tf_op jit(solution)/shard_map/while
  1384.7 42.4 %copy-start.7 = (f32[8,256]{1,0:T(8,128)S(1)}, f32[8,256]{1,0:T(8,128)}, u32[]{:S(2)}) copy-start(f32[8,256]{1,0:T(8,128)} %copy-done.6) | copy-start | bytes 24580 | tf_op jit(solution)/shard_map/while
  1427.1 59.9 %copy-start.6 = (f32[8,256]{1,0:T(8,128)}, f32[8,256]{1,0:T(8,128)S(1)}, u32[]{:S(2)}) copy-start(f32[8,256]{1,0:T(8,128)S(1)} %get-tuple-element.394) | copy-start | bytes 24580 | tf_op jit(solution)/shard_map/while
  1427.1 60.6 %copy-start.4 = (f32[8,256]{1,0:T(8,128)}, f32[8,256]{1,0:T(8,128)S(1)}, u32[]{:S(2)}) copy-start(f32[8,256]{1,0:T(8,128)S(1)} %get-tuple-element.399) | copy-start | bytes 24580 | tf_op jit(solution)/shard_map/while
  1604.5 42.4 %copy-start.7 = (f32[8,256]{1,0:T(8,128)S(1)}, f32[8,256]{1,0:T(8,128)}, u32[]{:S(2)}) copy-start(f32[8,256]{1,0:T(8,128)} %copy-done.6) | copy-start | bytes 24580 | tf_op jit(solution)/shard_map/while
  1646.9 59.8 %copy-start.6 = (f32[8,256]{1,0:T(8,128)}, f32[8,256]{1,0:T(8,128)S(1)}, u32[]{:S(2)}) copy-start(f32[8,256]{1,0:T(8,128)S(1)} %get-tuple-element.394) | copy-start | bytes 24580 | tf_op jit(solution)/shard_map/while
  1646.9 60.6 %copy-start.4 = (f32[8,256]{1,0:T(8,128)}, f32[8,256]{1,0:T(8,128)S(1)}, u32[]{:S(2)}) copy-start(f32[8,256]{1,0:T(8,128)S(1)} %get-tuple-element.399) | copy-start | bytes 24580 | tf_op jit(solution)/shard_map/while
  1824.3 42.4 %copy-start.5 = (f32[8,256]{1,0:T(8,128)S(1)}, f32[8,256]{1,0:T(8,128)}, u32[]{:S(2)}) copy-start(f32[8,256]{1,0:T(8,128)} %copy-done.4) | copy-start | bytes 24580 | tf_op jit(solution)/shard_map/while
  1824.3 42.4 %copy-start.7 = (f32[8,256]{1,0:T(8,128)S(1)}, f32[8,256]{1,0:T(8,128)}, u32[]{:S(2)}) copy-start(f32[8,256]{1,0:T(8,128)} %copy-done.6) | copy-start | bytes 24580 | tf_op jit(solution)/shard_map/while
  1866.7 59.8 %copy-start.6 = (f32[8,256]{1,0:T(8,128)}, f32[8,256]{1,0:T(8,128)S(1)}, u32[]{:S(2)}) copy-start(f32[8,256]{1,0:T(8,128)S(1)} %get-tuple-element.394) | copy-start | bytes 24580 | tf_op jit(solution)/shard_map/while
  1866.7 60.6 %copy-start.4 = (f32[8,256]{1,0:T(8,128)}, f32[8,256]{1,0:T(8,128)S(1)}, u32[]{:S(2)}) copy-start(f32[8,256]{1,0:T(8,128)S(1)} %get-tuple-element.399) | copy-start | bytes 24580 | tf_op jit(solution)/shard_map/while
  2044.1 42.4 %copy-start.5 = (f32[8,256]{1,0:T(8,128)S(1)}, f32[8,256]{1,0:T(8,128)}, u32[]{:S(2)}) copy-start(f32[8,256]{1,0:T(8,128)} %copy-done.4) | copy-start | bytes 24580 | tf_op jit(solution)/shard_map/while
  2044.1 42.4 %copy-start.7 = (f32[8,256]{1,0:T(8,128)S(1)}, f32[8,256]{1,0:T(8,128)}, u32[]{:S(2)}) copy-start(f32[8,256]{1,0:T(8,128)} %copy-done.6) | copy-start | bytes 24580 | tf_op jit(solution)/shard_map/while
  (23 other events, 463.5 us)
Sparse Core Ops, SparseCore 0:
  9.8 365.1 all-gather.1
  2086.7 1044.5 reduce-scatter.1
where the time goes:
time: 3140 us
  matrix products  1540 us (49%)
  waiting for transfers between devices  1290 us (41%)
  other arithmetic  184 us (6%)
  blocking collectives  72.2 us (2%)
  local copies, waits for them, and re-layouts  36.3 us (1%)
    reduce_scatter x1, waiting for transfers between devices, local(): lax.psum_scatter(grad_full, 'fsdp', scatter_dimension=0, tiled=True)  1000 us
    dot_general x8, matrix products, step(): lax.dot_general(d_logits, x_block, (((0,), (0,)), ((), ())), preferred_el...  872 us
    dot_general x8, matrix products, step(): lax.dot_general(x_block, emb_full, (((1,), (1,)), ((), ())), preferred_el...  344 us
    dot_general x8, matrix products, step(): dx_block = jnp.dot(d_logits, emb_full, preferred_element_type=jnp.float32)  328 us
    all_gather x1, waiting for transfers between devices, local(): emb_full = lax.all_gather(embedding, 'fsdp', tiled=True)  284 us
    reduce_sum x8, other arithmetic, step(): jnp.sum(jnp.where(is_target, logits, 0.0), axis=1)  129 us
  transfers between devices with their start and end apart: 2, of which 2 were waited for; matrix products, arithmetic and copies ran while one was open for 2% of the time, Pallas kernels for 0%

commit v1 on v0

v1 whole, which is shorter than its diff:
```python
import functools

import jax
import jax.numpy as jnp
from jax import lax
from jax.experimental import pallas as pl
from jax.experimental.pallas import tpu as pltpu
from jax.sharding import PartitionSpec as P

GROUP_SIZE = 8
CLIP_LOW = 0.8
CLIP_HIGH = 1.28
KL_COEF = 0.04
EPSILON = 1e-6

AXIS = 'fsdp'
N_DEV = 8
HALF = 256
BLK = 2 * HALF
N_J = 8
N_BLK = 4 * N_J
N_CHUNK = 5
SLAB = 16
N_SEND = 3
MESH = pl.DeviceIdType.MESH


def token_terms(tok_logp, old_block, ref_block, adv_block):
    ratio = jnp.exp(tok_logp - old_block)
    surr_raw = ratio * adv_block
    surr_clip = jnp.clip(ratio, CLIP_LOW, CLIP_HIGH) * adv_block
    kl_gap = ref_block - tok_logp
    tok_loss = -jnp.minimum(surr_raw, surr_clip) + KL_COEF * (jnp.exp(kl_gap) - kl_gap - 1.0)
    keep = (surr_raw <= surr_clip) | ((ratio > CLIP_LOW) & (ratio < CLIP_HIGH))
    d_logp = -jnp.where(keep, surr_raw, 0.0) + KL_COEF * (1.0 - jnp.exp(kl_gap))
    return tok_loss, d_logp


def bcast_kernel(x_ref, o_ref, send_sem, recv_sem):
    me = lax.axis_index(AXIS)
    barrier = pltpu.get_barrier_semaphore()
    for r in range(1, N_DEV):
        pl.semaphore_signal(barrier, inc=1, device_id=((me + r) % N_DEV,), device_id_type=MESH)
    pl.semaphore_wait(barrier, N_DEV - 1)
    copies = []
    for r in range(1, N_DEV):
        copies.append(pltpu.make_async_remote_copy(
            src_ref=x_ref, dst_ref=o_ref.at[me], send_sem=send_sem.at[r - 1], recv_sem=recv_sem.at[r - 1],
            device_id=((me + r) % N_DEV,), device_id_type=MESH))
    for c in copies:
        c.start()
    o_ref[me] = x_ref[...]
    for c in copies:
        c.wait()


def bcast_all(x, cid):
    return pl.pallas_call(
        bcast_kernel,
        out_shape=jax.ShapeDtypeStruct((N_DEV,) + x.shape, x.dtype),
        in_specs=[pl.BlockSpec(memory_space=pltpu.VMEM)],
        out_specs=pl.BlockSpec(memory_space=pltpu.VMEM),
        scratch_shapes=[pltpu.SemaphoreType.DMA((N_DEV - 1,)), pltpu.SemaphoreType.DMA((N_DEV - 1,))],
        compiler_params=pltpu.CompilerParams(collective_id=cid, has_side_effects=True),
        name=f'bcast{cid}',
    )(x)


def place(me):
    core = me % 2
    xpos = (me // 2) % 2
    ypos = me // 4
    par = (xpos + ypos) % 2
    pos = 2 * ypos + par
    partner = me + 1 - 2 * core
    xn = me + 2 - 4 * xpos
    yn = me + 4 - 8 * ypos
    nbr = ((1 - par) * xn + par * yn, par * xn + (1 - par) * yn)
    return core, me // 2, par, pos, partner, nbr


def logits_kernel(toki_ref, xown_hbm, e_hbm, xall_hbm, z_hbm, parts_ref,
                  e, z0, z1, xb0, xb1, acc, st,
                  e_sem, z_sem, xb_sem, oo_sem, ps, pr, ns, nr, fs, fr, qs, qr, ds, dr, ss, sr):
    vocab, dim = e_hbm.shape
    rows = vocab // N_CHUNK
    me = lax.axis_index(AXIS)
    core, chip, par_chip, pos, partner, nbr = place(me)
    diag_chip = 3 - chip
    diag = 2 * diag_chip + core
    zb = (z0, z1)
    xb = (xb0, xb1)

    barrier = pltpu.get_barrier_semaphore()
    for r in range(1, N_DEV):
        pl.semaphore_signal(barrier, inc=1, device_id=((me + r) % N_DEV,), device_id_type=MESH)
    pl.semaphore_wait(barrier, N_DEV - 1)

    def send(src, dst, ssem, rsem, dev):
        return pltpu.make_async_remote_copy(src_ref=src, dst_ref=dst, send_sem=ssem, recv_sem=rsem, device_id=(dev,), device_id_type=MESH)

    def to_partner(j):
        return send(xown_hbm.at[j], xall_hbm.at[me, j], ps.at[j], pr.at[j], partner)

    def to_nbr(side, j):
        return send(xown_hbm.at[j], xall_hbm.at[me, j], ns.at[side, j], nr.at[1 - side, j], nbr[side])

    def onward(side, j):
        ref = xall_hbm.at[nbr[1 - side], j]
        return send(ref, ref, fs.at[j], fr.at[j], nbr[side])

    def share_nbr(side, j):
        ref = xall_hbm.at[nbr[side], j]
        return send(ref, ref, qs.at[side, j], qr.at[side, j], partner)

    def share_diag(j):
        ref = xall_hbm.at[diag, j]
        return send(ref, ref, ds.at[j], dr.at[j], partner)

    def stats_group(g):
        return (chip, nbr[0] // 2, nbr[1] // 2, diag_chip)[g]

    def send_stats(r, g):
        rng = pl.ds(stats_group(g) * N_J, N_J)
        return send(st.at[rng], parts_ref.at[me, rng], ss.at[r - 1, g], sr.at[r - 1, g], (me + r) % N_DEV)

    e_copy = pltpu.make_async_copy(e_hbm, e, e_sem)
    e_copy.start()

    def load(par, half, src):
        return pltpu.make_async_copy(src, xb[par].at[half], xb_sem.at[par, half])

    def keep(par, j):
        return pltpu.make_async_copy(xb[par].at[core], xall_hbm.at[me, j], oo_sem.at[par])

    load(0, core, xown_hbm.at[0]).start()

    def first_sends(j, _):
        to_partner(j).start()
        to_nbr(0, j).start()
        to_nbr(1, j).start()
        return 0

    lax.fori_loop(0, N_J, first_sends, 0)
    to_partner(0).wait_recv()
    load(0, 1 - core, xall_hbm.at[partner, 0]).start()
    e_copy.wait()

    sub = lax.broadcasted_iota(jnp.int32, (SLAB, BLK), 0)

    def block_of(tt, par):
        a = tt // 4
        own = (3 - a) // 3
        far = a // 3
        near = 1 - own - far
        o = own * chip + near * (nbr[par] // 2) + far * diag_chip
        return o * N_J + own * (2 * tt + par) + near * (tt - 4) + far * (tt - 12 + 4 * par)

    def prefetch(tt, par):
        @pl.when(tt < 4)
        def _():
            j = 2 * tt + par
            load(par, core, xown_hbm.at[j]).start()
            to_partner(j).wait_recv()
            load(par, 1 - core, xall_hbm.at[partner, j]).start()

        @pl.when((tt >= 4) & (tt < 12))
        def _():
            j = tt - 4
            load(par, core, xall_hbm.at[nbr[par], j]).start()
            share_nbr(par, j).wait_recv()
            load(par, 1 - core, xall_hbm.at[nbr[par] + 1 - 2 * core, j]).start()

        @pl.when(tt >= 12)
        def _():
            j = tt - 12 + 4 * par
            load(par, core, xall_hbm.at[diag, j]).start()
            share_diag(j).wait_recv()
            load(par, 1 - core, xall_hbm.at[diag + 1 - 2 * core, j]).start()

    def z_out(blk, par):
        return pltpu.make_async_copy(zb[par], z_hbm.at[blk], z_sem.at[par])

    def dot(par, v, x):
        zb[par][v * rows:(v + 1) * rows, :] = lax.dot_general(
            e[v * rows:(v + 1) * rows, :], x, (((1,), (1,)), ((), ())), preferred_element_type=jnp.float32)

    def stats(par, v, rel, m, s, zt):
        cm = m
        for a in range(rows // SLAB):
            r0 = v * rows + a * SLAB
            cm = jnp.maximum(cm, zb[par][r0:r0 + SLAB, :])
        s = s * jnp.exp(m - cm)
        for a in range(rows // SLAB):
            r0 = v * rows + a * SLAB
            z = zb[par][r0:r0 + SLAB, :]
            s = s + jnp.exp(z - cm)
            zt = zt + jnp.where(rel == r0, z, 0.0)
        return cm, s, zt

    def close(par, blk):
        rel = jnp.broadcast_to(toki_ref[blk, 0:1, :], (SLAB, BLK)) - sub
        m, s, zt = stats(par, N_CHUNK - 1, rel, acc[0], acc[1], acc[2])
        top = jnp.max(m, axis=0, keepdims=True)
        st[blk, 0:1, :] = top + jnp.log(jnp.sum(s * jnp.exp(m - top), axis=0, keepdims=True))
        st[blk, 1:2, :] = jnp.sum(zt, axis=0, keepdims=True)

    def pair(tt, _):
        for par in (0, 1):
            other = 1 - par
            blk = block_of(tt, par)
            if par == 1:
                @pl.when((tt >= 1) & (tt < 9))
                def _():
                    j = tt - 1
                    for side in (0, 1):
                        to_nbr(1 - side, j).wait_recv()
                    for side in (0, 1):
                        share_nbr(side, j).start()

                    @pl.when(j < 4)
                    def _():
                        onward(0, j).start()

                    @pl.when(j >= 4)
                    def _():
                        onward(1, j).start()

                @pl.when((tt >= 10) & (tt < 14))
                def _():
                    for half in (0, 4):
                        onward(0, tt - 10 + half).wait_recv()
                        share_diag(tt - 10 + half).start()

                @pl.when(tt == 4)
                def _():
                    for r in range(1, N_DEV):
                        send_stats(r, 0).start()

                @pl.when(tt == 12)
                def _():
                    for r in range(1, N_DEV):
                        send_stats(r, 1).start()
                        send_stats(r, 2).start()

            for half in (0, 1):
                load(par, half, xown_hbm.at[0]).wait()

            @pl.when(tt < 4)
            def _():
                keep(par, 2 * tt + par).start()

            if par == 0:
                @pl.when((tt >= 1) & (tt < 5))
                def _():
                    keep(1, 0).wait()

                prefetch(tt, 1)
            else:
                @pl.when(tt < 4)
                def _():
                    keep(0, 0).wait()

                @pl.when(tt < 15)
                def _():
                    prefetch(tt + 1, 0)

            @pl.when(tt >= 1)
            def _():
                z_out(blk, par).wait()

            x = xb[par][...].reshape(BLK, dim)
            dot(par, 0, x)
            close(other, block_of(tt, 0) if par == 1 else block_of((tt + 15) % 16, 1))
            rel = jnp.broadcast_to(toki_ref[blk, 0:1, :], (SLAB, BLK)) - sub
            m = jnp.full((SLAB, BLK), -jnp.inf, jnp.float32)
            s = jnp.zeros((SLAB, BLK), jnp.float32)
            zt = s
            for v in range(1, N_CHUNK):
                dot(par, v, x)
                m, s, zt = stats(par, v - 1, rel, m, s, zt)
            acc[0] = m
            acc[1] = s
            acc[2] = zt
            z_out(blk, par).start()
        return 0

    lax.fori_loop(0, N_BLK // 2, pair, 0)
    close(1, block_of(15, 1))
    for r in range(1, N_DEV):
        send_stats(r, 3).start()
    parts_ref[me] = st[...]

    def drain(j, _):
        to_partner(j).wait_send()
        for side in (0, 1):
            to_nbr(side, j).wait_send()
            share_nbr(side, j).wait_send()
        onward(0, j).wait_send()
        share_diag(j).wait_send()
        return 0

    lax.fori_loop(0, N_J, drain, 0)
    for par in (0, 1):
        z_out(0, par).wait()
    for r in range(1, N_DEV):
        for g in range(4):
            send_stats(r, g).wait()


def logits_pass(toki, x_own, emb):
    vocab, dim = emb.shape
    vm = pltpu.VMEM
    dma = pltpu.SemaphoreType.DMA
    any_spec = pl.BlockSpec(memory_space=pl.ANY)
    vmem_spec = pl.BlockSpec(memory_space=pltpu.VMEM)
    return pl.pallas_call(
        logits_kernel,
        in_specs=[vmem_spec, any_spec, any_spec],
        out_specs=[any_spec, any_spec, vmem_spec],
        out_shape=[
            jax.ShapeDtypeStruct((N_DEV, N_J, HALF, dim), jnp.bfloat16),
            jax.ShapeDtypeStruct((N_BLK, vocab, BLK), jnp.float32),
            jax.ShapeDtypeStruct((N_DEV, N_BLK, 2, BLK), jnp.float32),
        ],
        scratch_shapes=[
            vm((vocab, dim), jnp.bfloat16), vm((vocab, BLK), jnp.float32), vm((vocab, BLK), jnp.float32),
            vm((2, HALF, dim), jnp.bfloat16), vm((2, HALF, dim), jnp.bfloat16),
            vm((3, SLAB, BLK), jnp.float32), vm((N_BLK, 2, BLK), jnp.float32),
            dma, dma((2,)), dma((2, 2)), dma((2,)),
            dma((N_J,)), dma((N_J,)), dma((2, N_J)), dma((2, N_J)), dma((N_J,)), dma((N_J,)),
            dma((2, N_J)), dma((2, N_J)), dma((N_J,)), dma((N_J,)), dma((N_DEV - 1, 4)), dma((N_DEV - 1, 4)),
        ],
        compiler_params=pltpu.CompilerParams(collective_id=1, has_side_effects=True, vmem_limit_bytes=60_000_000),
        cost_estimate=pl.CostEstimate(flops=2 * N_BLK * BLK * vocab * dim, bytes_accessed=4 * N_BLK * BLK * vocab, transcendentals=0),
        name='logits_pass',
    )(toki, x_own, emb)


def grad_kernel(tokf_ref, toki_ref, x_hbm, z_hbm, et_hbm, de_hbm, dx_hbm, ring_hbm,
                et, de, dz0, dz1, zb, xb0, xb1, dx0, dx1, d2d0, d2d1, rb0, rb1, sb,
                et_sem, x_sem, z_sem, d2d_ssem, d2d_rsem, ring_ssem, ring_rsem, rb_sem, out_sem, de_sem):
    dim, vocab = et_hbm.shape
    rows = vocab // N_CHUNK
    mrow = dim // N_CHUNK
    me = lax.axis_index(AXIS)
    core, chip, par, pos, partner, nbr = place(me)
    dz = (dz0, dz1)
    xb = (xb0, xb1)
    dx = (dx0, dx1)
    d2d = (d2d0, d2d1)
    rb = (rb0, rb1)

    barrier = pltpu.get_barrier_semaphore()
    for peer in (partner, nbr[0], nbr[1]):
        pl.semaphore_signal(barrier, inc=1, device_id=(peer,), device_id_type=MESH)
    pl.semaphore_wait(barrier, 3)

    def owner_of(stream, slot):
        p = (pos + 3 - slot) % 4 if stream == 0 else (pos + 1 + slot) % 4
        yy = p // 2
        return 2 * yy + (p % 2 + yy) % 2

    def block_of(stream, cnt):
        return owner_of(stream, cnt // 4) * N_J + 4 * stream + cnt % 4

    def x_copy(stream, cnt):
        o = owner_of(stream, cnt // 4)
        return pltpu.make_async_copy(x_hbm.at[pl.ds(2 * o, 2), 4 * stream + cnt % 4], xb[stream], x_sem.at[stream])

    def z_copy(g, slot):
        t = (g // N_CHUNK) % N_BLK
        cnt = t // 2
        odd = t % 2
        blk = (1 - odd) * block_of(0, cnt) + odd * block_of(1, cnt)
        part = g % N_CHUNK
        return pltpu.make_async_copy(z_hbm.at[blk, pl.ds(pl.multiple_of(part * rows, 8), rows)], zb.at[slot], z_sem.at[slot])

    et_copy = pltpu.make_async_copy(et_hbm, et, et_sem)
    z_copy(0, 0).start()
    z_copy(1, 1).start()
    et_copy.start()
    x_copy(0, 0).start()

    sub = lax.broadcasted_iota(jnp.int32, (SLAB, BLK), 0)

    def make_dz(dst, blk, v, slot):
        lse = jnp.broadcast_to(tokf_ref[blk, 0:1, :], (SLAB, BLK))
        coef = jnp.broadcast_to(tokf_ref[blk, 1:2, :], (SLAB, BLK))
        rel = jnp.broadcast_to(toki_ref[blk, 0:1, :], (SLAB, BLK)) - sub - v * rows
        for a in range(rows // SLAB):
            p = jnp.exp(zb[slot, a * SLAB:(a + 1) * SLAB, :] - lse)
            hot = jnp.where(rel == a * SLAB, 1.0, 0.0)
            dst[pl.ds(pl.multiple_of(v * rows + a * SLAB, SLAB), SLAB), :] = (coef * (hot - p)).astype(jnp.bfloat16)

    def first(v, _):
        slot = v % 2
        z_copy(v, slot).wait()
        make_dz(dz0, block_of(0, 0), v, slot)
        z_copy(v + 2, slot).start()
        return 0

    lax.fori_loop(0, N_CHUNK, first, 0)

    def clear(r, _):
        de[pl.ds(pl.multiple_of(r * 80, 8), 80), :] = jnp.zeros((80, dim), jnp.float32)
        return 0

    lax.fori_loop(0, vocab // 80, clear, 0)
    et_copy.wait()

    def d2d_copy(stream):
        return pltpu.make_async_remote_copy(
            src_ref=dx[stream].at[1 - core], dst_ref=d2d[stream], send_sem=d2d_ssem.at[stream], recv_sem=d2d_rsem.at[stream],
            device_id=(partner,), device_id_type=MESH)

    def ring_copy(stream, cnt, buf):
        return pltpu.make_async_remote_copy(
            src_ref=sb.at[stream, buf], dst_ref=ring_hbm.at[stream, cnt], send_sem=ring_ssem.at[stream, buf], recv_sem=ring_rsem.at[stream, cnt],
            device_id=(nbr[stream],), device_id_type=MESH)

    def fetch_copy(stream, cnt):
        return pltpu.make_async_copy(ring_hbm.at[stream, cnt], rb[stream], rb_sem.at[stream])

    def out_copy(stream, i, buf):
        return pltpu.make_async_copy(sb.at[stream, buf], dx_hbm.at[4 * stream + i], out_sem.at[stream, buf])

    def finish(stream, cnt):
        buf = cnt % N_SEND
        d2d_copy(stream).wait()

        @pl.when((cnt >= N_SEND) & (cnt < 12 + N_SEND))
        def _():
            ring_copy(stream, 0, buf).wait_send()

        @pl.when(cnt >= 12 + N_SEND)
        def _():
            out_copy(stream, 0, buf).wait()

        def add(r, with_ring):
            sl = pl.ds(pl.multiple_of(r * 64, 8), 64)
            val = dx[stream][core, sl, :] + d2d[stream][sl, :]
            if with_ring:
                val = val + rb[stream][sl, :]
            sb[stream, buf, sl, :] = val
            return 0

        @pl.when(cnt < 4)
        def _():
            lax.fori_loop(0, dim // 64, lambda r, c: add(r, False), 0)

        @pl.when(cnt >= 4)
        def _():
            fetch_copy(stream, cnt - 4).wait()
            lax.fori_loop(0, dim // 64, lambda r, c: add(r, True), 0)

        @pl.when(cnt < 12)
        def _():
            ring_copy(stream, cnt, buf).start()

        @pl.when(cnt >= 12)
        def _():
            out_copy(stream, cnt - 12, buf).start()

    def pair(cnt, _):
        for stream in (0, 1):
            t = 2 * cnt + stream
            other = 1 - stream
            x_copy(stream, cnt).wait()
            if stream == 0:
                x_copy(1, cnt).start()
                nblk = block_of(1, cnt)
            else:
                @pl.when(cnt < 15)
                def _():
                    x_copy(0, cnt + 1).start()
                nblk = block_of(0, (cnt + 1) % 16)

            def chunk(v, _):
                g = (t + 1) * N_CHUNK + v
                slot = g % 2
                z_copy(g, slot).wait()
                xv = xb[stream][...].reshape(BLK, dim)
                sl = pl.ds(pl.multiple_of(v * rows, SLAB), rows)
                de[sl, :] += jnp.dot(dz[stream][sl, :], xv, preferred_element_type=jnp.float32)
                ml = pl.ds(pl.multiple_of(v * mrow, 16), mrow)
                part = jnp.dot(et[ml, :], dz[stream][...], preferred_element_type=jnp.float32)
                dx[stream][0, ml, :] = part[:, :HALF]
                dx[stream][1, ml, :] = part[:, HALF:]
                make_dz(dz[other], nblk, v, slot)
                z_copy(g + 2, slot).start()
                return 0

            lax.fori_loop(0, N_CHUNK, chunk, 0)

            if stream == 1:
                finish(0, cnt)
            else:
                @pl.when(cnt > 0)
                def _():
                    finish(1, cnt - 1)
            d2d_copy(stream).start()

            @pl.when(cnt >= 4)
            def _():
                ring_copy(stream, cnt - 4, 0).wait_recv()
                fetch_copy(stream, cnt - 4).start()
        return 0

    lax.fori_loop(0, 16, pair, 0)
    de_copy = pltpu.make_async_copy(de, de_hbm, de_sem)
    de_copy.start()
    finish(1, 15)
    for stream in (0, 1):
        for cnt in range(16 - N_SEND, 16):
            out_copy(stream, 0, cnt % N_SEND).wait()
    last = (N_BLK + 1) * N_CHUNK
    for g in (last, last + 1):
        z_copy(g, g % 2).wait()
    de_copy.wait()


def grad_pass(tokf, toki, x_all, z_all, emb_t):
    dim, vocab = emb_t.shape
    rows = vocab // N_CHUNK
    f32 = jnp.float32
    vm = pltpu.VMEM
    dma = pltpu.SemaphoreType.DMA
    piece = (dim, HALF)
    return pl.pallas_call(
        grad_kernel,
        in_specs=[pl.BlockSpec(memory_space=pltpu.VMEM)] * 2 + [pl.BlockSpec(memory_space=pl.ANY)] * 3,
        out_specs=[pl.BlockSpec(memory_space=pl.ANY)] * 3,
        out_shape=[
            jax.ShapeDtypeStruct((vocab, dim), f32),
            jax.ShapeDtypeStruct((N_J,) + piece, f32),
            jax.ShapeDtypeStruct((2, 12) + piece, f32),
        ],
        scratch_shapes=[
            vm((dim, vocab), jnp.bfloat16), vm((vocab, dim), f32),
            vm((vocab, BLK), jnp.bfloat16), vm((vocab, BLK), jnp.bfloat16),
            vm((2, rows, BLK), f32),
            vm((2, HALF, dim), jnp.bfloat16), vm((2, HALF, dim), jnp.bfloat16),
            vm((2,) + piece, f32), vm((2,) + piece, f32),
            vm(piece, f32), vm(piece, f32), vm(piece, f32), vm(piece, f32),
            vm((2, N_SEND) + piece, f32),
            dma, dma((2,)), dma((2,)), dma((2,)), dma((2,)), dma((2, N_SEND)), dma((2, 12)), dma((2,)), dma((2, N_SEND)), dma,
        ],
        compiler_params=pltpu.CompilerParams(collective_id=2, has_side_effects=True, vmem_limit_bytes=67_000_000),
        cost_estimate=pl.CostEstimate(flops=4 * N_BLK * BLK * vocab * dim, bytes_accessed=4 * N_BLK * BLK * vocab, transcendentals=0),
        name='grad_pass',
    )(tokf, toki, x_all, z_all, emb_t)


def solution(mesh):
    shards = mesh.shape[AXIS]

    def local(hidden, targets, resp_mask, resp_id, old_logp, ref_logp, rewards, prompt_id, norm_w, embedding):
        tok_dev, dim = hidden.shape
        vocab = embedding.shape[0]
        n_resp = rewards.shape[0]
        prompts = n_resp * shards // GROUP_SIZE
        me = lax.axis_index(AXIS)
        f32 = jnp.float32

        pieces = [targets.astype(f32), resp_mask.astype(f32), resp_id.astype(f32), old_logp, ref_logp]
        tail = jnp.concatenate([rewards, prompt_id.astype(f32), norm_w.astype(f32)])
        tail = jnp.pad(tail, (0, 1024 - tail.shape[0]))
        small = jnp.concatenate(pieces + [tail]).reshape(-1, 128)
        every = bcast_all(small, 0).reshape(shards, -1)
        tgt, mask_f, rid, old, ref = [every[:, i * tok_dev:(i + 1) * tok_dev] for i in range(5)]
        tail = every[:, 5 * tok_dev:]
        rew = tail[:, :n_resp]
        pid = tail[:, n_resp:2 * n_resp].astype(jnp.int32)
        gain = tail[:, 2 * n_resp:2 * n_resp + norm_w.shape[0]].reshape(dim)

        hid_f32 = hidden.astype(f32)
        inv_rms = lax.rsqrt(jnp.mean(hid_f32 * hid_f32, axis=-1, keepdims=True) + EPSILON)
        normed = hid_f32 * inv_rms
        x_rows = (normed * gain).astype(jnp.bfloat16)

        same = (pid.reshape(-1)[:, None] == jnp.arange(prompts, dtype=jnp.int32)[None, :])
        flat = rew.reshape(-1)[:, None]
        tot1 = jnp.sum(jnp.where(same, flat, 0.0), axis=0)
        tot2 = jnp.sum(jnp.where(same, flat * flat, 0.0), axis=0)
        cnt = jnp.sum(jnp.where(same, 1.0, 0.0), axis=0)
        mean_r = tot1 / cnt
        std_r = jnp.sqrt(jnp.maximum(tot2 / cnt - mean_r * mean_r, 0.0))
        mean_t = jnp.sum(jnp.where(same, mean_r[None, :], 0.0), axis=1)
        std_t = jnp.sum(jnp.where(same, std_r[None, :], 0.0), axis=1)
        adv = ((rew.reshape(-1) - mean_t) / (std_t + EPSILON)).reshape(shards, n_resp)
        hit = rid[:, None, :] == jnp.arange(n_resp, dtype=f32)[None, :, None]
        adv_tok = jnp.sum(jnp.where(hit, adv[:, :, None], 0.0), axis=1)
        count = jnp.sum(mask_f)

        def order(a):
            return a.reshape(shards // 2, 2, N_J, HALF).transpose(0, 2, 1, 3).reshape(N_BLK, BLK)

        tgt_loc = order(tgt).astype(jnp.int32) - me * vocab
        toki = jnp.broadcast_to(tgt_loc[:, None, :], (N_BLK, 8, BLK))

        x_all, z_all, parts = logits_pass(toki, x_rows.reshape(N_J, HALF, dim), embedding)
        lses = parts[:, :, 0]
        top = jnp.max(lses, axis=0)
        lse = top + jnp.log(jnp.sum(jnp.exp(lses - top), axis=0))
        tok_logp = jnp.sum(parts[:, :, 1], axis=0) - lse
        mask_b = order(mask_f)
        tok_loss, d_logp = token_terms(tok_logp, order(old), order(ref), order(adv_tok))
        coef = mask_b * d_logp / count
        mean_loss = jnp.sum(mask_b * tok_loss) / count
        tokf = jnp.concatenate([lse[:, None], coef[:, None], jnp.zeros((N_BLK, 6, BLK), f32)], axis=1)

        d_embedding, dx_t, _ = grad_pass(tokf, toki, x_all, z_all, embedding.T)
        d_x = dx_t.transpose(0, 2, 1).reshape(tok_dev, dim)
        dg_part = jnp.pad(jnp.sum(d_x * normed, axis=0), (0, 2048 - dim)).reshape(16, 128)
        dg_all = jnp.sum(bcast_all(dg_part, 3), axis=0).reshape(-1)[:dim].reshape(shards, dim // shards)
        d_norm_w = lax.dynamic_index_in_dim(dg_all, me, 0, keepdims=False)
        d_normed = d_x * gain
        d_hidden = (inv_rms * (d_normed - normed * jnp.mean(d_normed * normed, axis=-1, keepdims=True))).astype(jnp.bfloat16)
        return mean_loss, d_hidden, d_embedding, d_norm_w

    tok_spec = P(AXIS)
    row_spec = P(AXIS, None)
    return jax.shard_map(local, mesh=mesh, in_specs=(row_spec, tok_spec, tok_spec, tok_spec, tok_spec, tok_spec, tok_spec, tok_spec, tok_spec, row_spec), out_specs=(P(), row_spec, row_spec, tok_spec), check_vma=False)
```

time: 3140 us -> 789 us (0.25)
  matrix products: 1540 us -> 0 us
  waiting for transfers between devices: 1290 us -> 0 us
  Pallas kernels: 0 us -> 696 us
  other arithmetic: 184 us -> 36.9 us
  blocking collectives: 72.2 us -> 0 us
    dot_general x24 -> x0, matrix products: 1540 us -> none  [the longest x8 872 us: step(): lax.dot_general(d_logits, x_block, (((0,), (0,)), ((), ())), preferred_el...]
    reduce_scatter x1 -> x0, waiting for transfers between devices: 1000 us -> none  [local(): lax.psum_scatter(grad_full, 'fsdp', scatter_dimension=0, tiled=True)]
    pallas_call x0 -> x4, Pallas kernels: none -> 696 us  [the longest x1 447 us: grad_pass(): pl.pallas_call(grad_kernel, in_specs=[pl.BlockSpec(memory_space=pltpu.VME...]
    all_gather x1 -> x0, waiting for transfers between devices: 284 us -> none  [local(): emb_full = lax.all_gather(embedding, 'fsdp', tiled=True)]
    reduce_sum x18 -> x7, other arithmetic: 142 us -> 2.73 us  [the longest x1 0.85 us: local(): jnp.sum(bcast_all(dg_part, 3), axis=0).reshape(-1)[:dim]]
    psum x2 -> x0, blocking collectives: 48 us -> none  [the longest x1 25.5 us: local(): lax.psum(jax.ops.segment_sum(rew_stats, prompt_id, num_segments=prompts),...]
  transfers between devices with their start and end apart: 2 -> 0, of which waited for: 2 -> 0; matrix products, arithmetic and copies ran while one was open for 2% -> 0% of each run, Pallas kernels for 0% -> 0%
where the time goes in v1:
time: 789 us; the launch traced here: 788 us
  Pallas kernels  696 us (88%)
  local copies, waits for them, and re-layouts  50.9 us (6%)
  other arithmetic  36.9 us (5%)
    pallas_call x1, Pallas kernels, grad_pass(): pl.pallas_call(grad_kernel, in_specs=[pl.BlockSpec(memory_space=pltpu.VME...  447 us
    pallas_call x1, Pallas kernels, logits_pass(): pl.pallas_call(logits_kernel, in_specs=[vmem_spec, any_spec, any_spec], o...  232 us
    unnamed x48, local copies, waits for them, and re-layouts  33.5 us
    pallas_call x2, Pallas kernels, bcast_all(): pl.pallas_call(bcast_kernel, out_shape=jax.ShapeDtypeStruct((N_DEV,) + x....  17.1 us

profile of v1, /device:TPU:0, one launch (start us, length us, event | category | flops | bytes accessed | tf_op | source)
XLA Modules:
  0.0 787.7 jit_solution(2419439692066163694)
XLA Ops:
  0.6 0.7 convert_element_type.44
  1.9 0.7 convert_element_type.45
  2.6 3.6 fusion.10
  6.2 0.7 convert_dynamic-update-slice_fusion.2
  6.9 0.7 convert_dynamic-update-slice_fusion.1
  7.6 0.7 convert_dynamic-update-slice_fusion
  8.3 0.7 constant_dynamic-update-slice_fusion.1
  9.0 0.7 constant_dynamic-update-slice_fusion
  9.7 0.7 fusion.19
  10.4 0.6 copy-done.17
  11.0 10.8 %bcast0.1 = f32[8,88,128]{2,1,0:T(8,128)} custom-call(f32[88,128]{1,0:T(8,128)} %bitcast.83), custom_call_target="tpu_custom_call" | custom-call | tf_op jit(solution)/shard_map/bcast0/pallas_call | solution.py:58
  21.9 1.1 copy.47
  23.8 0.6 slice_reduce_fusion.1
  25.5 0.7 reshape.254
  26.3 0.7 reshape.255
  27.0 0.7 reshape.256
  27.8 0.7 reshape.257
  28.5 0.8 broadcast_in_dim.77.toki_ref
  29.4 6.1 fusion.4
  35.5 14.1 %copy.33 = bf16[4000,1280]{0,1:T(8,128)(2,1)} copy(bf16[4000,1280]{1,0:T(8,128)(2,1)} %e_hbm.1) | data formatting | bytes 20480000 | tf_op args[9]
  49.7 232.0 %logits_pass.1 = (bf16[8,8,256,1280]{3,2,1,0:T(8,128)(2,1)}, f32[32,4000,512]{2,1,0:T(8,128)}, f32[8,32,2,512]{3,2,1,0:T(2,128)}) custom-call(s32[32,8,512]{2,1,0:T(8,128)} %broadcast_in_dim.77.toki_ref, bf16[8,256,1280]{2,1,0:T(8,128)(2,1)} %bitcast.60, bf16[4000,1280]{1,0:T(8,128)(2,1)} %e_hbm.1), custom_call_target="tpu_custom_call" | custom-call | flops 167772160000 | bytes 262144000 | tf_op jit(solution)/shard_map/logits_pass/pallas_call | solution.py:317
  281.7 2.8 slice_reduce_fusion.2
  284.7 1.0 multiply_divide_fusion
  285.7 0.6 fusion.17
  287.8 0.9 maximum_maximum_fusion.tokf_ref
  288.7 447.4 %grad_pass.1 = (f32[4000,1280]{1,0:T(8,128)}, f32[8,1280,256]{2,1,0:T(8,128)}, f32[2,12,1280,256]{3,2,1,0:T(8,128)}) custom-call(f32[32,8,512]{2,1,0:T(8,128)} %maximum_maximum_fusion.tokf_ref, s32[32,8,512]{2,1,0:T(8,128)} %broadcast_in_dim.77.toki_ref, bf16[8,8,256,1280]{3,2,1,0:T(8,128)(2,1)} %get-tuple-element.10.x_hbm, ...), custom_call_target="tpu_custom_call" | custom-call | flops 335544320000 | bytes 262144000 | tf_op jit(solution)/shard_map/grad_pass/pallas_call | solution.py:530
  736.1 11.2 %copy.34 = f32[8,256,1280]{2,1,0:T(8,128)} copy(f32[8,256,1280]{1,2,0:T(8,128)} %bitcast.58) | data formatting | bytes 20971520 | tf_op jit(solution)/shard_map/transpose | solution.py:614
  747.4 8.3 %fusion.9 = (f32[1280]{0:T(1024)S(1)}, f32[2048]{0:T(1024)S(1)}) fusion(bf16[2048,1280]{1,0:T(8,128)(2,1)} %param.10, f32[8,256,1280]{2,1,0:T(8,128)} %copy.34, f32[2048]{0:T(1024)S(1)} %copy-done.14, f32[1280]{0:T(1024)S(1)} %copy-done.16), kind=kLoop, calls=%fused_computation.11 | loop fusion | flops 18346752 | bytes 15755264 | tf_op jit(solution)/shard_map/reduce_sum | solution.py:615
  756.2 7.1 fusion.8
  763.3 6.2 bcast3.1
  769.6 0.9 reduce_sum.145
  771.1 15.5 %copy.54 = f32[4000,1280]{1,0:T(8,128)} copy(f32[4000,1280]{1,0:T(8,128)} %get-tuple-element.41) | data formatting | bytes 40960000
  (71 shorter events, 4.1 us)
Async XLA Ops:
  6.2 43.5 %copy-start.13 = (f32[2048]{0:T(1024)}, f32[2048]{0:T(1024)S(1)}, u32[]{:S(2)}) copy-start(f32[2048]{0:T(1024)S(1)} %add_rsqrt_fusion) | copy-start | bytes 24580
  10.4 0.6 copy-start.17
  23.1 26.5 %copy-start.15 = (f32[1280]{0:T(1024)}, f32[1280]{0:T(1024)S(1)}, u32[]{:S(2)}) copy-start(f32[1280]{0:T(1024)S(1)} %mul.123) | copy-start | bytes 15364
  24.4 25.2 %copy-start.1 = (f32[1,8,8,256]{3,2,1,0:T(8,128)}, f32[1,8,8,256]{3,2,1,0:T(8,128)S(1)}, u32[]{:S(2)}) copy-start(f32[1,8,8,256]{3,2,1,0:T(8,128)S(1)} %copy.41) | copy-start | bytes 196612
  24.8 24.8 %copy-start.3 = (f32[1,8,8,256]{3,2,1,0:T(8,128)}, f32[1,8,8,256]{3,2,1,0:T(8,128)S(1)}, u32[]{:S(2)}) copy-start(f32[1,8,8,256]{3,2,1,0:T(8,128)S(1)} %copy.40) | copy-start | bytes 196612
  24.8 24.8 %copy-start.5 = (f32[1,8,8,256]{3,2,1,0:T(8,128)}, f32[1,8,8,256]{3,2,1,0:T(8,128)S(1)}, u32[]{:S(2)}) copy-start(f32[1,8,8,256]{3,2,1,0:T(8,128)S(1)} %copy.39) | copy-start | bytes 196612
  24.9 0.6 copy-start.7
  49.6 235.0 %copy-start.9 = (f32[32,1,512]{2,1,0:T(1,128)S(1)}, f32[32,1,512]{2,1,0:T(1,128)}, u32[]{:S(2)}) copy-start(f32[32,1,512]{2,1,0:T(1,128)} %reshape.254) | copy-start | bytes 196612
  49.7 235.0 %copy-start.10 = (f32[32,1,512]{2,1,0:T(1,128)S(1)}, f32[32,1,512]{2,1,0:T(1,128)}, u32[]{:S(2)}) copy-start(f32[32,1,512]{2,1,0:T(1,128)} %reshape.255) | copy-start | bytes 196612
  49.7 235.0 %copy-start.11 = (f32[32,1,512]{2,1,0:T(1,128)S(1)}, f32[32,1,512]{2,1,0:T(1,128)}, u32[]{:S(2)}) copy-start(f32[32,1,512]{2,1,0:T(1,128)} %reshape.256) | copy-start | bytes 196612
  49.7 235.0 %copy-start.12 = (f32[32,1,512]{2,1,0:T(1,128)S(1)}, f32[32,1,512]{2,1,0:T(1,128)}, u32[]{:S(2)}) copy-start(f32[32,1,512]{2,1,0:T(1,128)} %reshape.257) | copy-start | bytes 196612
  49.7 236.0 %copy-start.2 = (f32[1,8,8,256]{3,2,1,0:T(8,128)S(1)}, f32[1,8,8,256]{3,2,1,0:T(8,128)}, u32[]{:S(2)}) copy-start(f32[1,8,8,256]{3,2,1,0:T(8,128)} %copy-done.1) | copy-start | bytes 196612
  49.7 236.0 %copy-start.4 = (f32[1,8,8,256]{3,2,1,0:T(8,128)S(1)}, f32[1,8,8,256]{3,2,1,0:T(8,128)}, u32[]{:S(2)}) copy-start(f32[1,8,8,256]{3,2,1,0:T(8,128)} %copy-done.3) | copy-start | bytes 196612
  49.7 236.0 %copy-start.6 = (f32[1,8,8,256]{3,2,1,0:T(8,128)S(1)}, f32[1,8,8,256]{3,2,1,0:T(8,128)}, u32[]{:S(2)}) copy-start(f32[1,8,8,256]{3,2,1,0:T(8,128)} %copy-done.5) | copy-start | bytes 196612
  49.7 236.0 %copy-start.8 = (f32[1,8,8,256]{3,2,1,0:T(8,128)S(1)}, f32[1,8,8,256]{3,2,1,0:T(8,128)}, u32[]{:S(2)}) copy-start(f32[1,8,8,256]{3,2,1,0:T(8,128)} %copy-done.7) | copy-start | bytes 196612
  49.7 238.1 %copy-start.18 = (f32[8]{0:T(128)S(1)}, f32[8]{0:T(128)}, u32[]{:S(2)}) copy-start(f32[8]{0:T(128)} %pad.12.clone) | copy-start | bytes 100
  736.1 11.3 %copy-start.14 = (f32[2048]{0:T(1024)S(1)}, f32[2048]{0:T(1024)}, u32[]{:S(2)}) copy-start(f32[2048]{0:T(1024)} %copy-done.13) | copy-start | bytes 24580
  736.1 11.2 %copy-start.16 = (f32[1280]{0:T(1024)S(1)}, f32[1280]{0:T(1024)}, u32[]{:S(2)}) copy-start(f32[1280]{0:T(1024)} %copy-done.15) | copy-start | bytes 15364
  747.4 8.9 %copy-start = (f32[8,256,1280]{2,1,0:T(8,128)S(1)}, f32[8,256,1280]{2,1,0:T(8,128)}, u32[]{:S(2)}) copy-start(f32[8,256,1280]{2,1,0:T(8,128)} %copy.34) | copy-start | bytes 31457284

commit v2 on v1

--- a/solution.py
+++ b/solution.py
@@ -15,14 +15,32 @@
 
 AXIS = 'fsdp'
 N_DEV = 8
+PEERS = range(1, N_DEV)
+N_PEER = len(PEERS)
+PAIR = (0, 1)
+ORIGIN = (0, 0, 0)
+NONE = 0
+SIDE_VMEM = 48_000_000
 HALF = 256
 BLK = 2 * HALF
+LANES = 128
 N_J = 8
 N_BLK = 4 * N_J
 N_CHUNK = 5
 SLAB = 16
 N_SEND = 3
+N_PIECE = 2
+SLABS_E = (12, 12)
+SLABS_X = (6, 6, 6, 8)
+N_LOGIT = 10
+K_PART = 1024
 MESH = pl.DeviceIdType.MESH
+NT_DIMS = (((1,), (1,)), ((), ()))
+PARAMS = functools.partial(pltpu.CompilerParams, has_side_effects=True)
+
+
+row_mean = functools.partial(jnp.mean, axis=-1, keepdims=True)
+col_sum = functools.partial(jnp.sum, axis=0, keepdims=True)
 
 
 def token_terms(tok_logp, old_block, ref_block, adv_block):
@@ -39,11 +57,11 @@
 def bcast_kernel(x_ref, o_ref, send_sem, recv_sem):
     me = lax.axis_index(AXIS)
     barrier = pltpu.get_barrier_semaphore()
-    for r in range(1, N_DEV):
-        pl.semaphore_signal(barrier, inc=1, device_id=((me + r) % N_DEV,), device_id_type=MESH)
-    pl.semaphore_wait(barrier, N_DEV - 1)
+    for r in PEERS:
+        pl.semaphore_signal(barrier, device_id=((me + r) % N_DEV,), device_id_type=MESH)
+    pl.semaphore_wait(barrier, N_PEER)
     copies = []
-    for r in range(1, N_DEV):
+    for r in PEERS:
         copies.append(pltpu.make_async_remote_copy(
             src_ref=x_ref, dst_ref=o_ref.at[me], send_sem=send_sem.at[r - 1], recv_sem=recv_sem.at[r - 1],
             device_id=((me + r) % N_DEV,), device_id_type=MESH))
@@ -60,8 +78,8 @@
         out_shape=jax.ShapeDtypeStruct((N_DEV,) + x.shape, x.dtype),
         in_specs=[pl.BlockSpec(memory_space=pltpu.VMEM)],
         out_specs=pl.BlockSpec(memory_space=pltpu.VMEM),
-        scratch_shapes=[pltpu.SemaphoreType.DMA((N_DEV - 1,)), pltpu.SemaphoreType.DMA((N_DEV - 1,))],
-        compiler_params=pltpu.CompilerParams(collective_id=cid, has_side_effects=True),
+        scratch_shapes=[pltpu.SemaphoreType.DMA((N_PEER,)), pltpu.SemaphoreType.DMA((N_PEER,))],
+        compiler_params=PARAMS(collective_id=cid),
         name=f'bcast{cid}',
     )(x)
 
@@ -79,22 +97,21 @@
     return core, me // 2, par, pos, partner, nbr
 
 
-def logits_kernel(toki_ref, xown_hbm, e_hbm, xall_hbm, z_hbm, parts_ref,
-                  e, z0, z1, xb0, xb1, acc, st,
-                  e_sem, z_sem, xb_sem, oo_sem, ps, pr, ns, nr, fs, fr, qs, qr, ds, dr, ss, sr):
+def logits_kernel(toki_ref, xown_hbm, e_hbm, xall_hbm, z_hbm, parts_ref, et_hbm,
+                  e, zb, xb0, xb1, acc, st, eb,
+                  eb_sem, e_sem, z_sem, xb_sem, oo_sem, ps, pr, ns, nr, fs, fr, qs, qr, ds, dr, ss, sr):
     vocab, dim = e_hbm.shape
-    rows = vocab // N_CHUNK
+    rows = vocab // N_LOGIT
     me = lax.axis_index(AXIS)
     core, chip, par_chip, pos, partner, nbr = place(me)
     diag_chip = 3 - chip
     diag = 2 * diag_chip + core
-    zb = (z0, z1)
     xb = (xb0, xb1)
 
     barrier = pltpu.get_barrier_semaphore()
-    for r in range(1, N_DEV):
-        pl.semaphore_signal(barrier, inc=1, device_id=((me + r) % N_DEV,), device_id_type=MESH)
-    pl.semaphore_wait(barrier, N_DEV - 1)
+    for r in PEERS:
+        pl.semaphore_signal(barrier, device_id=((me + r) % N_DEV,), device_id_type=MESH)
+    pl.semaphore_wait(barrier, N_PEER)
 
     def send(src, dst, ssem, rsem, dev):
         return pltpu.make_async_remote_copy(src_ref=src, dst_ref=dst, send_sem=ssem, recv_sem=rsem, device_id=(dev,), device_id_type=MESH)
@@ -124,7 +141,8 @@
         rng = pl.ds(stats_group(g) * N_J, N_J)
         return send(st.at[rng], parts_ref.at[me, rng], ss.at[r - 1, g], sr.at[r - 1, g], (me + r) % N_DEV)
 
-    e_copy = pltpu.make_async_copy(e_hbm, e, e_sem)
+    e_copy = pltpu.make_async_copy(e_hbm, e.at[pl.ds(0, vocab)], e_sem)
+    e[vocab:, :] = jnp.zeros((e.shape[0] - vocab, dim), jnp.bfloat16)
     e_copy.start()
 
     def load(par, half, src):
@@ -179,43 +197,46 @@
             load(par, 1 - core, xall_hbm.at[diag + 1 - 2 * core, j]).start()
 
     def z_out(blk, par):
-        return pltpu.make_async_copy(zb[par], z_hbm.at[blk], z_sem.at[par])
-
-    def dot(par, v, x):
-        zb[par][v * rows:(v + 1) * rows, :] = lax.dot_general(
-            e[v * rows:(v + 1) * rows, :], x, (((1,), (1,)), ((), ())), preferred_element_type=jnp.float32)
-
-    def stats(par, v, rel, m, s, zt):
+        return pltpu.make_async_copy(zb.at[pl.ds(par * vocab, vocab)], z_hbm.at[blk], z_sem.at[par])
+
+    def part_of(base, q, a):
+        return pl.ds(pl.multiple_of(base + q * rows + a * SLAB, SLAB), SLAB)
+
+    def et_out(t, par):
+        return pltpu.make_async_copy(eb.at[par], et_hbm.at[:, pl.ds(pl.multiple_of(t * LANES, LANES), LANES)], eb_sem.at[par])
+
+    def dot(base, q, x):
+        zb[pl.ds(pl.multiple_of(base + q * rows, SLAB), rows), :] = lax.dot_general(
+            e[q * rows:(q + 1) * rows, :], x, NT_DIMS, preferred_element_type=jnp.float32)
+
+    def stats(base, q, rel, m, s, zt):
         cm = m
         for a in range(rows // SLAB):
-            r0 = v * rows + a * SLAB
-            cm = jnp.maximum(cm, zb[par][r0:r0 + SLAB, :])
+            cm = jnp.maximum(cm, zb[part_of(base, q, a), :])
         s = s * jnp.exp(m - cm)
         for a in range(rows // SLAB):
-            r0 = v * rows + a * SLAB
-            z = zb[par][r0:r0 + SLAB, :]
+            z = zb[part_of(base, q, a), :]
             s = s + jnp.exp(z - cm)
-            zt = zt + jnp.where(rel == r0, z, 0.0)
+            zt = zt + jnp.where(rel == q * rows + a * SLAB, z, 0.0)
         return cm, s, zt
 
-    def close(par, blk):
+    def close(base, blk):
         rel = jnp.broadcast_to(toki_ref[blk, 0:1, :], (SLAB, BLK)) - sub
-        m, s, zt = stats(par, N_CHUNK - 1, rel, acc[0], acc[1], acc[2])
+        m, s, zt = stats(base, N_LOGIT - 1, rel, acc[0], acc[1], acc[2])
         top = jnp.max(m, axis=0, keepdims=True)
-        st[blk, 0:1, :] = top + jnp.log(jnp.sum(s * jnp.exp(m - top), axis=0, keepdims=True))
-        st[blk, 1:2, :] = jnp.sum(zt, axis=0, keepdims=True)
+        st[blk, 0:1, :] = top + jnp.log(col_sum(s * jnp.exp(m - top)))
+        st[blk, 1:2, :] = col_sum(zt)
 
     def pair(tt, _):
-        for par in (0, 1):
-            other = 1 - par
+        for par in PAIR:
             blk = block_of(tt, par)
             if par == 1:
-                @pl.when((tt >= 1) & (tt < 9))
-                def _():
-                    j = tt - 1
-                    for side in (0, 1):
+                @pl.when((tt >= 2) & (tt < 10))
+                def _():
+                    j = tt - 2
+                    for side in PAIR:
                         to_nbr(1 - side, j).wait_recv()
-                    for side in (0, 1):
+                    for side in PAIR:
                         share_nbr(side, j).start()
 
                     @pl.when(j < 4)
@@ -234,16 +255,16 @@
 
                 @pl.when(tt == 4)
                 def _():
-                    for r in range(1, N_DEV):
+                    for r in PEERS:
                         send_stats(r, 0).start()
 
                 @pl.when(tt == 12)
                 def _():
-                    for r in range(1, N_DEV):
+                    for r in PEERS:
                         send_stats(r, 1).start()
                         send_stats(r, 2).start()
 
-            for half in (0, 1):
+            for half in PAIR:
                 load(par, half, xown_hbm.at[0]).wait()
 
             @pl.when(tt < 4)
@@ -268,32 +289,38 @@
             @pl.when(tt >= 1)
             def _():
                 z_out(blk, par).wait()
+                et_out(0, par).wait()
 
             x = xb[par][...].reshape(BLK, dim)
-            dot(par, 0, x)
-            close(other, block_of(tt, 0) if par == 1 else block_of((tt + 15) % 16, 1))
+            t = 2 * tt + par
+            cur = (5 * t) % 2 * vocab
+            same = cur + me // N_DEV * SLAB
+            dot(cur, 0, x)
+            eb[par] = e[pl.ds(pl.multiple_of(t * LANES, LANES), LANES), :].T
+            close((5 * t + 5) % 2 * vocab + me // N_DEV * SLAB, block_of(tt, 0) if par == 1 else block_of((tt + 15) % 16, 1))
             rel = jnp.broadcast_to(toki_ref[blk, 0:1, :], (SLAB, BLK)) - sub
             m = jnp.full((SLAB, BLK), -jnp.inf, jnp.float32)
             s = jnp.zeros((SLAB, BLK), jnp.float32)
             zt = s
-            for v in range(1, N_CHUNK):
-                dot(par, v, x)
-                m, s, zt = stats(par, v - 1, rel, m, s, zt)
+            for q in range(1, N_LOGIT):
+                dot(cur, q, x)
+                m, s, zt = stats(same, q - 1, rel, m, s, zt)
             acc[0] = m
             acc[1] = s
             acc[2] = zt
             z_out(blk, par).start()
+            et_out(t, par).start()
         return 0
 
     lax.fori_loop(0, N_BLK // 2, pair, 0)
-    close(1, block_of(15, 1))
-    for r in range(1, N_DEV):
+    close(vocab, block_of(15, 1))
+    for r in PEERS:
         send_stats(r, 3).start()
     parts_ref[me] = st[...]
 
     def drain(j, _):
         to_partner(j).wait_send()
-        for side in (0, 1):
+        for side in PAIR:
             to_nbr(side, j).wait_send()
             share_nbr(side, j).wait_send()
         onward(0, j).wait_send()
@@ -301,9 +328,10 @@
         return 0
 
     lax.fori_loop(0, N_J, drain, 0)
-    for par in (0, 1):
+    for par in PAIR:
         z_out(0, par).wait()
-    for r in range(1, N_DEV):
+        et_out(0, par).wait()
+    for r in PEERS:
         for g in range(4):
             send_stats(r, g).wait()
 
@@ -312,40 +340,43 @@
     vocab, dim = emb.shape
     vm = pltpu.VMEM
     dma = pltpu.SemaphoreType.DMA
+    two = dma((2,))
     any_spec = pl.BlockSpec(memory_space=pl.ANY)
     vmem_spec = pl.BlockSpec(memory_space=pltpu.VMEM)
     return pl.pallas_call(
         logits_kernel,
         in_specs=[vmem_spec, any_spec, any_spec],
-        out_specs=[any_spec, any_spec, vmem_spec],
+        out_specs=[any_spec, any_spec, vmem_spec, any_spec],
         out_shape=[
             jax.ShapeDtypeStruct((N_DEV, N_J, HALF, dim), jnp.bfloat16),
             jax.ShapeDtypeStruct((N_BLK, vocab, BLK), jnp.float32),
             jax.ShapeDtypeStruct((N_DEV, N_BLK, 2, BLK), jnp.float32),
+            jax.ShapeDtypeStruct((dim, N_BLK * LANES), jnp.bfloat16),
         ],
         scratch_shapes=[
-            vm((vocab, dim), jnp.bfloat16), vm((vocab, BLK), jnp.float32), vm((vocab, BLK), jnp.float32),
-            vm((2, HALF, dim), jnp.bfloat16), vm((2, HALF, dim), jnp.bfloat16),
-            vm((3, SLAB, BLK), jnp.float32), vm((N_BLK, 2, BLK), jnp.float32),
-            dma, dma((2,)), dma((2, 2)), dma((2,)),
-            dma((N_J,)), dma((N_J,)), dma((2, N_J)), dma((2, N_J)), dma((N_J,)), dma((N_J,)),
-            dma((2, N_J)), dma((2, N_J)), dma((N_J,)), dma((N_J,)), dma((N_DEV - 1, 4)), dma((N_DEV - 1, 4)),
+            vm((N_BLK * LANES, dim), jnp.bfloat16), vm((2 * vocab, BLK), jnp.float32),
+            *[vm((2, HALF, dim), jnp.bfloat16)] * 2,
+            vm((3, SLAB, BLK), jnp.float32), vm((N_BLK, 2, BLK), jnp.float32), vm((2, dim, LANES), jnp.bfloat16),
+            two, dma, two, dma((2, 2)), two,
+            dma((N_J,)), dma((N_J,)), *[dma((2, N_J))] * 2, dma((N_J,)), dma((N_J,)),
+            *[dma((2, N_J))] * 2, dma((N_J,)), dma((N_J,)), dma((N_PEER, 4)), dma((N_PEER, 4)),
         ],
-        compiler_params=pltpu.CompilerParams(collective_id=1, has_side_effects=True, vmem_limit_bytes=60_000_000),
-        cost_estimate=pl.CostEstimate(flops=2 * N_BLK * BLK * vocab * dim, bytes_accessed=4 * N_BLK * BLK * vocab, transcendentals=0),
+        compiler_params=PARAMS(collective_id=1, vmem_limit_bytes=60_000_000),
+        cost_estimate=pl.CostEstimate(flops=2 * N_BLK * BLK * vocab * dim, bytes_accessed=4 * N_BLK * BLK * vocab, transcendentals=NONE),
         name='logits_pass',
     )(toki, x_own, emb)
 
 
-def grad_kernel(tokf_ref, toki_ref, x_hbm, z_hbm, et_hbm, de_hbm, dx_hbm, ring_hbm,
-                et, de, dz0, dz1, zb, xb0, xb1, dx0, dx1, d2d0, d2d1, rb0, rb1, sb,
-                et_sem, x_sem, z_sem, d2d_ssem, d2d_rsem, ring_ssem, ring_rsem, rb_sem, out_sem, de_sem):
-    dim, vocab = et_hbm.shape
+def grad_kernel(tokf_ref, toki_ref, x_hbm, z_hbm, et_hbm, de_hbm, dx_hbm, ring_hbm, dz_hbm, xl_hbm,
+                et, de, dz, zb, xb0, xb1, dx0, dx1, d2d0, d2d1, rb0, rb1, sb,
+                et_sem, x_sem, z_sem, d2d_ssem, d2d_rsem, ring_ssem, ring_rsem, rb_sem, out_sem, de_sem, held_sem):
+    dim, vocab = et_hbm.shape[0], z_hbm.shape[1]
     rows = vocab // N_CHUNK
     mrow = dim // N_CHUNK
+    piece = rows // N_PIECE
+    n_slab = rows // SLAB
     me = lax.axis_index(AXIS)
     core, chip, par, pos, partner, nbr = place(me)
-    dz = (dz0, dz1)
     xb = (xb0, xb1)
     dx = (dx0, dx1)
     d2d = (d2d0, d2d1)
@@ -353,7 +384,7 @@
 
     barrier = pltpu.get_barrier_semaphore()
     for peer in (partner, nbr[0], nbr[1]):
-        pl.semaphore_signal(barrier, inc=1, device_id=(peer,), device_id_type=MESH)
+        pl.semaphore_signal(barrier, device_id=(peer,), device_id_type=MESH)
     pl.semaphore_wait(barrier, 3)
 
     def owner_of(stream, slot):
@@ -384,19 +415,19 @@
 
     sub = lax.broadcasted_iota(jnp.int32, (SLAB, BLK), 0)
 
-    def make_dz(dst, blk, v, slot):
+    def make_dz(base, blk, v, slot, slabs):
         lse = jnp.broadcast_to(tokf_ref[blk, 0:1, :], (SLAB, BLK))
         coef = jnp.broadcast_to(tokf_ref[blk, 1:2, :], (SLAB, BLK))
         rel = jnp.broadcast_to(toki_ref[blk, 0:1, :], (SLAB, BLK)) - sub - v * rows
-        for a in range(rows // SLAB):
+        for a in slabs:
             p = jnp.exp(zb[slot, a * SLAB:(a + 1) * SLAB, :] - lse)
             hot = jnp.where(rel == a * SLAB, 1.0, 0.0)
-            dst[pl.ds(pl.multiple_of(v * rows + a * SLAB, SLAB), SLAB), :] = (coef * (hot - p)).astype(jnp.bfloat16)
+            dz[pl.ds(pl.multiple_of(base + v * rows + a * SLAB, SLAB), SLAB), :] = (coef * (hot - p)).astype(jnp.bfloat16)
 
     def first(v, _):
         slot = v % 2
         z_copy(v, slot).wait()
-        make_dz(dz0, block_of(0, 0), v, slot)
+        make_dz(0, block_of(0, 0), v, slot, range(n_slab))
         z_copy(v + 2, slot).start()
         return 0
 
@@ -463,31 +494,42 @@
             out_copy(stream, cnt - 12, buf).start()
 
     def pair(cnt, _):
-        for stream in (0, 1):
+        for stream in PAIR:
             t = 2 * cnt + stream
-            other = 1 - stream
+            cur = (5 * t) % 2 * vocab
+            nxt = (5 * t + 5) % 2 * vocab
             x_copy(stream, cnt).wait()
             if stream == 0:
                 x_copy(1, cnt).start()
                 nblk = block_of(1, cnt)
             else:
-                @pl.when(cnt < 15)
-                def _():
-                    x_copy(0, cnt + 1).start()
-                nblk = block_of(0, (cnt + 1) % 16)
+                x_copy(0, cnt + 1).start()
+                nblk = block_of(0, cnt + 1)
 
             def chunk(v, _):
                 g = (t + 1) * N_CHUNK + v
                 slot = g % 2
                 z_copy(g, slot).wait()
                 xv = xb[stream][...].reshape(BLK, dim)
-                sl = pl.ds(pl.multiple_of(v * rows, SLAB), rows)
-                de[sl, :] += jnp.dot(dz[stream][sl, :], xv, preferred_element_type=jnp.float32)
                 ml = pl.ds(pl.multiple_of(v * mrow, 16), mrow)
-                part = jnp.dot(et[ml, :], dz[stream][...], preferred_element_type=jnp.float32)
+                cut = 0
+                for q in range(N_PIECE):
+                    sl = pl.ds(pl.multiple_of(v * rows + q * piece, SLAB), piece)
+                    lhs = dz[pl.ds(pl.multiple_of(cur + v * rows + q * piece, SLAB), piece), :]
+                    de[sl, :] += jnp.dot(lhs, xv, preferred_element_type=jnp.float32)
+                    make_dz(nxt, nblk, v, slot, range(cut, cut + SLABS_E[q]))
+                    cut += SLABS_E[q]
+                part = jnp.zeros((mrow, BLK), jnp.float32)
+                for q in range(len(SLABS_X)):
+                    lo = q * K_PART
+                    hi = min(lo + K_PART, vocab)
+                    rhs = dz[pl.ds(pl.multiple_of(cur + lo, SLAB), hi - lo), :]
+                    part = part + jnp.dot(et[ml, lo:hi], rhs, preferred_element_type=jnp.float32)
+                    make_dz(nxt, nblk, v, slot, range(cut, cut + SLABS_X[q]))
+                    cut += SLABS_X[q]
+                assert cut == n_slab
                 dx[stream][0, ml, :] = part[:, :HALF]
                 dx[stream][1, ml, :] = part[:, HALF:]
-                make_dz(dz[other], nblk, v, slot)
                 z_copy(g + 2, slot).start()
                 return 0
 
@@ -507,49 +549,153 @@
                 fetch_copy(stream, cnt - 4).start()
         return 0
 
-    lax.fori_loop(0, 16, pair, 0)
+    lax.fori_loop(0, 15, pair, 0)
     de_copy = pltpu.make_async_copy(de, de_hbm, de_sem)
     de_copy.start()
+    held = []
+    for stream in PAIR:
+        x_copy(stream, 15).wait()
+        if stream == 0:
+            x_copy(1, 15).start()
+        cur = stream * vocab
+        held.append(pltpu.make_async_copy(dz.at[pl.ds(cur, vocab)], dz_hbm.at[stream], held_sem.at[0, stream]))
+        held.append(pltpu.make_async_copy(xb[stream], xl_hbm.at[stream], held_sem.at[1, stream]))
+        for c in held[-2:]:
+            c.start()
+
+        def last_chunk(v, _):
+            ml = pl.ds(pl.multiple_of(v * mrow, 16), mrow)
+            part = jnp.dot(et[ml, :vocab], dz[cur:cur + vocab, :], preferred_element_type=jnp.float32)
+            dx[stream][0, ml, :] = part[:, :HALF]
+            dx[stream][1, ml, :] = part[:, HALF:]
+            if stream == 0:
+                g = 31 * N_CHUNK + v
+                slot = g % 2
+                z_copy(g, slot).wait()
+                make_dz(vocab, block_of(1, 15), v, slot, range(n_slab))
+
+                @pl.when(v < N_CHUNK - 2)
+                def _():
+                    z_copy(g + 2, slot).start()
+            return 0
+
+        lax.fori_loop(0, N_CHUNK, last_chunk, 0)
+        finish(1 - stream, 14 + stream)
+        d2d_copy(stream).start()
+        ring_copy(stream, 11, 0).wait_recv()
+        fetch_copy(stream, 11).start()
     finish(1, 15)
-    for stream in (0, 1):
+    for c in held:
+        c.wait()
+    for stream in PAIR:
         for cnt in range(16 - N_SEND, 16):
             out_copy(stream, 0, cnt % N_SEND).wait()
-    last = (N_BLK + 1) * N_CHUNK
-    for g in (last, last + 1):
-        z_copy(g, g % 2).wait()
     de_copy.wait()
 
 
 def grad_pass(tokf, toki, x_all, z_all, emb_t):
-    dim, vocab = emb_t.shape
+    dim, vocab = emb_t.shape[0], z_all.shape[1]
     rows = vocab // N_CHUNK
     f32 = jnp.float32
     vm = pltpu.VMEM
     dma = pltpu.SemaphoreType.DMA
+    two = dma((2,))
     piece = (dim, HALF)
+    by_buf = dma((2, N_SEND))
     return pl.pallas_call(
         grad_kernel,
         in_specs=[pl.BlockSpec(memory_space=pltpu.VMEM)] * 2 + [pl.BlockSpec(memory_space=pl.ANY)] * 3,
-        out_specs=[pl.BlockSpec(memory_space=pl.ANY)] * 3,
+        out_specs=[pl.BlockSpec(memory_space=pl.ANY)] * 5,
         out_shape=[
             jax.ShapeDtypeStruct((vocab, dim), f32),
             jax.ShapeDtypeStruct((N_J,) + piece, f32),
             jax.ShapeDtypeStruct((2, 12) + piece, f32),
+            jax.ShapeDtypeStruct((2, vocab, BLK), jnp.bfloat16),
+            jax.ShapeDtypeStruct((2, 2, HALF, dim), jnp.bfloat16),
         ],
         scratch_shapes=[
-            vm((dim, vocab), jnp.bfloat16), vm((vocab, dim), f32),
-            vm((vocab, BLK), jnp.bfloat16), vm((vocab, BLK), jnp.bfloat16),
+            vm(emb_t.shape, jnp.bfloat16), vm((vocab, dim), f32),
+            vm((2 * vocab, BLK), jnp.bfloat16),
             vm((2, rows, BLK), f32),
-            vm((2, HALF, dim), jnp.bfloat16), vm((2, HALF, dim), jnp.bfloat16),
-            vm((2,) + piece, f32), vm((2,) + piece, f32),
-            vm(piece, f32), vm(piece, f32), vm(piece, f32), vm(piece, f32),
+            *[vm((2, HALF, dim), jnp.bfloat16)] * 2,
+            *[vm((2,) + piece, f32)] * 2,
+            *[vm(piece, f32)] * 4,
             vm((2, N_SEND) + piece, f32),
-            dma, dma((2,)), dma((2,)), dma((2,)), dma((2,)), dma((2, N_SEND)), dma((2, 12)), dma((2,)), dma((2, N_SEND)), dma,
+            dma, two, two, two, two, by_buf, dma((2, 12)), two, by_buf, dma, dma((2, 2)),
         ],
-        compiler_params=pltpu.CompilerParams(collective_id=2, has_side_effects=True, vmem_limit_bytes=67_000_000),
-        cost_estimate=pl.CostEstimate(flops=4 * N_BLK * BLK * vocab * dim, bytes_accessed=4 * N_BLK * BLK * vocab, transcendentals=0),
+        compiler_params=PARAMS(collective_id=2, vmem_limit_bytes=67_000_000),
+        cost_estimate=pl.CostEstimate(flops=4 * N_BLK * BLK * vocab * dim, bytes_accessed=4 * N_BLK * BLK * vocab, transcendentals=NONE),
         name='grad_pass',
     )(tokf, toki, x_all, z_all, emb_t)
+
+
+def emb_kernel(part_ref, dz_ref, x_ref, o_ref):
+    acc = part_ref[...]
+    for b in PAIR:
+        acc = acc + jnp.dot(dz_ref[b], x_ref[b], preferred_element_type=jnp.float32)
+    o_ref[...] = acc
+
+
+def emb_pass(de_part, dz_last, x_last):
+    vocab, dim = de_part.shape
+    rows = vocab // 10
+    return pl.pallas_call(
+        emb_kernel,
+        grid=(10,),
+        in_specs=[
+            pl.BlockSpec((rows, dim), lambda i: (i, 0)),
+            pl.BlockSpec((2, rows, BLK), lambda i: (0, i, 0)),
+            pl.BlockSpec((2, BLK, dim), lambda i: ORIGIN),
+        ],
+        out_specs=pl.BlockSpec((rows, dim), lambda i: (i, 0)),
+        out_shape=jax.ShapeDtypeStruct((vocab, dim), jnp.float32),
+        compiler_params=pltpu.CompilerParams(vmem_limit_bytes=SIDE_VMEM),
+        cost_estimate=pl.CostEstimate(flops=4 * BLK * vocab * dim, bytes_accessed=8 * vocab * dim, transcendentals=NONE),
+        name='emb_pass',
+    )(de_part, dz_last, x_last)
+
+
+def norm_kernel(dx_ref, h_ref, g_ref, dh_ref, dg_ref):
+    dim = h_ref.shape[-1]
+    dx = dx_ref[0].T
+    hid = h_ref[0].astype(jnp.float32)
+    inv = lax.rsqrt(row_mean(hid * hid) + EPSILON)
+    n = hid * inv
+    part = jnp.sum((dx * n).reshape(HALF // 8, 8, dim), axis=0)
+
+    @pl.when(pl.program_id(0) == 0)
+    def _():
+        dg_ref[...] = part
+
+    @pl.when(pl.program_id(0) > 0)
+    def _():
+        dg_ref[...] += part
+
+    u = dx * g_ref[...]
+    dh_ref[0] = (inv * (u - n * row_mean(u * n))).astype(jnp.bfloat16)
+
+
+def norm_pass(dx_t, hid, gain):
+    n_j, dim, half = dx_t.shape
+    return pl.pallas_call(
+        norm_kernel,
+        grid=(n_j,),
+        in_specs=[
+            pl.BlockSpec((1, dim, half), lambda j: (j, 0, 0)),
+            pl.BlockSpec((1, half, dim), lambda j: (j, 0, 0)),
+            pl.BlockSpec((1, dim), lambda j: ORIGIN[1:]),
+        ],
+        out_specs=[
+            pl.BlockSpec((1, half, dim), lambda j: (j, 0, 0)),
+            pl.BlockSpec((8, dim), lambda j: ORIGIN[1:]),
+        ],
+        out_shape=[
+            jax.ShapeDtypeStruct((n_j, half, dim), jnp.bfloat16),
+            jax.ShapeDtypeStruct((8, dim), jnp.float32),
+        ],
+        compiler_params=pltpu.CompilerParams(vmem_limit_bytes=SIDE_VMEM),
+        name='norm_pass',
+    )(dx_t, hid, gain)
 
 
 def solution(mesh):
@@ -565,7 +711,7 @@
 
         pieces = [targets.astype(f32), resp_mask.astype(f32), resp_id.astype(f32), old_logp, ref_logp]
         tail = jnp.concatenate([rewards, prompt_id.astype(f32), norm_w.astype(f32)])
-        tail = jnp.pad(tail, (0, 1024 - tail.shape[0]))
+        tail = jnp.pad(tail, (0, 1024 - tail.size))
         small = jnp.concatenate(pieces + [tail]).reshape(-1, 128)
         every = bcast_all(small, 0).reshape(shards, -1)
         tgt, mask_f, rid, old, ref = [every[:, i * tok_dev:(i + 1) * tok_dev] for i in range(5)]
@@ -575,7 +721,7 @@
         gain = tail[:, 2 * n_resp:2 * n_resp + norm_w.shape[0]].reshape(dim)
 
         hid_f32 = hidden.astype(f32)
-        inv_rms = lax.rsqrt(jnp.mean(hid_f32 * hid_f32, axis=-1, keepdims=True) + EPSILON)
+        inv_rms = lax.rsqrt(row_mean(hid_f32 * hid_f32) + EPSILON)
         normed = hid_f32 * inv_rms
         x_rows = (normed * gain).astype(jnp.bfloat16)
 
@@ -599,7 +745,7 @@
         tgt_loc = order(tgt).astype(jnp.int32) - me * vocab
         toki = jnp.broadcast_to(tgt_loc[:, None, :], (N_BLK, 8, BLK))
 
-        x_all, z_all, parts = logits_pass(toki, x_rows.reshape(N_J, HALF, dim), embedding)
+        x_all, z_all, parts, emb_t = logits_pass(toki, x_rows.reshape(N_J, HALF, dim), embedding)
         lses = parts[:, :, 0]
         top = jnp.max(lses, axis=0)
         lse = top + jnp.log(jnp.sum(jnp.exp(lses - top), axis=0))
@@ -610,13 +756,13 @@
         mean_loss = jnp.sum(mask_b * tok_loss) / count
         tokf = jnp.concatenate([lse[:, None], coef[:, None], jnp.zeros((N_BLK, 6, BLK), f32)], axis=1)
 
-        d_embedding, dx_t, _ = grad_pass(tokf, toki, x_all, z_all, embedding.T)
-        d_x = dx_t.transpose(0, 2, 1).reshape(tok_dev, dim)
-        dg_part = jnp.pad(jnp.sum(d_x * normed, axis=0), (0, 2048 - dim)).reshape(16, 128)
+        de_part, dx_t, _, dz_last, x_last = grad_pass(tokf, toki, x_all, z_all, emb_t)
+        d_hidden, dg_rows = norm_pass(dx_t, hidden.reshape(N_J, HALF, dim), gain.reshape(1, dim))
+        d_hidden = d_hidden.reshape(tok_dev, dim)
+        dg_part = jnp.pad(jnp.sum(dg_rows, axis=0), (0, 2048 - dim)).reshape(16, 128)
+        d_embedding = emb_pass(de_part, dz_last, x_last.reshape(2, BLK, dim))
         dg_all = jnp.sum(bcast_all(dg_part, 3), axis=0).reshape(-1)[:dim].reshape(shards, dim // shards)
         d_norm_w = lax.dynamic_index_in_dim(dg_all, me, 0, keepdims=False)
-        d_normed = d_x * gain
-        d_hidden = (inv_rms * (d_normed - normed * jnp.mean(d_normed * normed, axis=-1, keepdims=True))).astype(jnp.bfloat16)
         return mean_loss, d_hidden, d_embedding, d_norm_w
 
     tok_spec = P(AXIS)

time: 789 us -> 744 us (0.943)
  local copies, waits for them, and re-layouts: 50.9 us -> 12 us
  other arithmetic: 36.9 us -> 22.4 us
  Pallas kernels: 696 us -> 705 us
    pallas_call x0 -> x2, Pallas kernels: none -> 35.2 us  [the longest x1 23.5 us: emb_pass(): pl.pallas_call(emb_kernel, grid=(10,), in_specs=[pl.BlockSpec((rows, dim)...]
    pallas_call x1, Pallas kernels: 447 us -> 419 us  [grad_pass(): pl.pallas_call(grad_kernel, in_specs=[pl.BlockSpec(memory_space=pltpu.VME...]
    unnamed x48 -> x32, local copies, waits for them, and re-layouts: 33.5 us -> 5.71 us
    transpose x1 -> x0, local copies, waits for them, and re-layouts: 11.2 us -> none  [local(): d_x = dx_t.transpose(0, 2, 1).reshape(tok_dev, dim)]
    reduce_sum x2, other arithmetic: 11.9 us -> 3.59 us  [the longest x1 3.58 us: local(): inv_rms = lax.rsqrt(row_mean(hid_f32 * hid_f32) + EPSILON)]
where the time goes in v2:
time: 744 us; the launch traced here: 743 us
  Pallas kernels  705 us (95%)
  other arithmetic  22.4 us (3%)
  local copies, waits for them, and re-layouts  12 us (2%)
    pallas_call x1, Pallas kernels, grad_pass(): pl.pallas_call(grad_kernel, in_specs=[pl.BlockSpec(memory_space=pltpu.VME...  419 us
    pallas_call x1, Pallas kernels, logits_pass(): pl.pallas_call(logits_kernel, in_specs=[vmem_spec, any_spec, any_spec], o...  233 us
    pallas_call x1, Pallas kernels, emb_pass(): pl.pallas_call(emb_kernel, grid=(10,), in_specs=[pl.BlockSpec((rows, dim)...  23.5 us
    pallas_call x2, Pallas kernels, bcast_all(): pl.pallas_call(bcast_kernel, out_shape=jax.ShapeDtypeStruct((N_DEV,) + x....  17 us

profile of v2, /device:TPU:0, one launch (start us, length us, event | category | flops | bytes accessed | tf_op | source)
XLA Modules:
  0.0 742.8 jit_solution(8106285923671914322)
XLA Ops:
  0.6 0.7 convert_element_type.41
  1.3 0.6 pad.12.clone
  1.9 0.7 convert_element_type.42
  2.6 3.6 fusion
  6.2 0.7 convert_dynamic-update-slice_fusion.2
  6.9 0.7 convert_dynamic-update-slice_fusion.1
  7.6 0.7 convert_dynamic-update-slice_fusion
  8.3 0.7 constant_dynamic-update-slice_fusion.1
  8.9 0.7 constant_dynamic-update-slice_fusion
  9.6 0.7 fusion.11
  10.4 0.6 copy-done.10
  11.0 10.8 %bcast0.1 = f32[8,88,128]{2,1,0:T(8,128)} custom-call(f32[88,128]{1,0:T(8,128)} %bitcast.77), custom_call_target="tpu_custom_call" | custom-call | tf_op jit(solution)/shard_map/bcast0/pallas_call | solution.py:76
  21.9 1.1 copy.42
  23.9 0.6 slice_reduce_fusion.1
  25.0 0.7 reshape.256
  25.8 0.7 reshape.257
  26.5 0.7 reshape.258
  27.3 0.7 reshape.259
  28.0 0.9 broadcast_in_dim.76.toki_ref
  28.8 6.1 fusion.2
  35.0 233.5 %logits_pass.1 = (bf16[8,8,256,1280]{3,2,1,0:T(8,128)(2,1)}, f32[32,4000,512]{2,1,0:T(8,128)}, f32[8,32,2,512]{3,2,1,0:T(2,128)}, bf16[1280,4096]{1,0:T(8,128)(2,1)}) custom-call(s32[32,8,512]{2,1,0:T(8,128)} %broadcast_in_dim.76.toki_ref, bf16[8,256,1280]{2,1,0:T(8,128)(2,1)} %bitcast.54, bf16[4000,1280]{1,0:T(8,128)(2,1)} %e_hbm.1), custom_call_target="tpu_custom_call" | custom-call | flops 167772160000 | bytes 262144000 | tf_op jit(solution)/shard_map/logits_pass/pallas_call | solution.py:346
  268.5 2.8 slice_reduce_fusion.2
  271.4 1.0 multiply_divide_fusion
  272.4 1.6 fusion.9
  275.4 0.9 maximum_maximum_fusion.tokf_ref
  276.4 419.3 %grad_pass.1 = (f32[4000,1280]{1,0:T(8,128)}, f32[8,1280,256]{2,1,0:T(8,128)}, f32[2,12,1280,256]{3,2,1,0:T(8,128)}, bf16[2,4000,512]{2,1,0:T(8,128)(2,1)}, bf16[2,2,256,1280]{3,2,1,0:T(8,128)(2,1)}) custom-call(f32[32,8,512]{2,1,0:T(8,128)} %maximum_maximum_fusion.tokf_ref, s32[32,8,512]{2,1,0:T(8,128)} %broadcast_in_dim.76.toki_ref, ...), custom_call_target="tpu_custom_call" | custom-call | flops 335544320000 | bytes 262144000 | tf_op jit(solution)/shard_map/grad_pass/pallas_call | solution.py:605
  695.7 2.5 copy-done
  698.2 11.7 %norm_pass.1 = (bf16[8,256,1280]{2,1,0:T(8,128)(2,1)}, f32[8,1280]{1,0:T(8,128)S(1)}) custom-call(f32[8,1280,256]{2,1,0:T(8,128)} %get-tuple-element.18.dx_ref, bf16[8,256,1280]{2,1,0:T(8,128)(2,1)S(1)} %bitcast.52, f32[1,1280]{1,0:T(1,128)S(1)} %broadcast_in_dim_reshape.2.g_ref), custom_call_target="tpu_custom_call" | custom-call | tf_op jit(solution)/shard_map/norm_pass/pallas_call | solution.py:680
  709.9 0.6 pad_bitcast_fusion.x_ref
  710.5 6.2 bcast3.1
  716.7 0.9 reduce_sum.135
  718.2 23.5 %emb_pass.1 = f32[4000,1280]{1,0:T(8,128)} custom-call(f32[4000,1280]{1,0:T(8,128)} %get-tuple-element.20.part_ref, bf16[2,4000,512]{2,1,0:T(8,128)(2,1)} %get-tuple-element.21.dz_ref, bf16[2,512,1280]{2,1,0:T(8,128)(2,1)S(1)} %bitcast.53), custom_call_target="tpu_custom_call" | custom-call | flops 10485760000 | bytes 40960000 | tf_op jit(solution)/shard_map/emb_pass/pallas_call | solution.py:642
  (55 shorter events, 2.3 us)
Async XLA Ops:
  10.4 0.6 copy-start.10
  24.5 243.9 %copy-start.2 = (f32[1,8,8,256]{3,2,1,0:T(8,128)}, f32[1,8,8,256]{3,2,1,0:T(8,128)S(1)}, u32[]{:S(2)}) copy-start(f32[1,8,8,256]{3,2,1,0:T(8,128)S(1)} %copy.36) | copy-start | bytes 196612
  24.9 243.6 %copy-start.3 = (f32[1,8,8,256]{3,2,1,0:T(8,128)}, f32[1,8,8,256]{3,2,1,0:T(8,128)S(1)}, u32[]{:S(2)}) copy-start(f32[1,8,8,256]{3,2,1,0:T(8,128)S(1)} %copy.35) | copy-start | bytes 196612
  24.9 243.5 %copy-start.4 = (f32[1,8,8,256]{3,2,1,0:T(8,128)}, f32[1,8,8,256]{3,2,1,0:T(8,128)S(1)}, u32[]{:S(2)}) copy-start(f32[1,8,8,256]{3,2,1,0:T(8,128)S(1)} %copy.34) | copy-start | bytes 196612
  25.0 243.5 %copy-start.5 = (f32[1,8,8,256]{3,2,1,0:T(8,128)}, f32[1,8,8,256]{3,2,1,0:T(8,128)S(1)}, u32[]{:S(2)}) copy-start(f32[1,8,8,256]{3,2,1,0:T(8,128)S(1)} %copy.32) | copy-start | bytes 196612
  34.9 236.4 %copy-start.6 = (f32[32,1,512]{2,1,0:T(1,128)S(1)}, f32[32,1,512]{2,1,0:T(1,128)}, u32[]{:S(2)}) copy-start(f32[32,1,512]{2,1,0:T(1,128)} %reshape.256) | copy-start | bytes 196612
  34.9 236.4 %copy-start.7 = (f32[32,1,512]{2,1,0:T(1,128)S(1)}, f32[32,1,512]{2,1,0:T(1,128)}, u32[]{:S(2)}) copy-start(f32[32,1,512]{2,1,0:T(1,128)} %reshape.257) | copy-start | bytes 196612
  34.9 236.4 %copy-start.8 = (f32[32,1,512]{2,1,0:T(1,128)S(1)}, f32[32,1,512]{2,1,0:T(1,128)}, u32[]{:S(2)}) copy-start(f32[32,1,512]{2,1,0:T(1,128)} %reshape.258) | copy-start | bytes 196612
  34.9 236.4 %copy-start.9 = (f32[32,1,512]{2,1,0:T(1,128)S(1)}, f32[32,1,512]{2,1,0:T(1,128)}, u32[]{:S(2)}) copy-start(f32[32,1,512]{2,1,0:T(1,128)} %reshape.259) | copy-start | bytes 196612
  35.0 240.5 %copy-start.11 = (f32[8]{0:T(128)S(1)}, f32[8]{0:T(128)}, u32[]{:S(2)}) copy-start(f32[8]{0:T(128)} %pad.12.clone) | copy-start | bytes 100
  695.7 2.5 copy-start
  698.2 20.0 %copy-start.1 = (bf16[2,2,256,1280]{3,2,1,0:T(8,128)(2,1)S(1)}, bf16[2,2,256,1280]{3,2,1,0:T(8,128)(2,1)}, u32[]{:S(2)}) copy-start(bf16[2,2,256,1280]{3,2,1,0:T(8,128)(2,1)} %get-tuple-element.22) | copy-start | bytes 7864324
